TPU v7x, 32 devices: a 4x2x2 block of a 4x4x8 slice. The times are simulated.
32 devices in a mesh: dp: 4 (over y, z), tp: 8 (over x, core).
Axes of the slice: x: 4, y: 2, z: 2, core: 2. Of those that a mesh axis runs over, the one named last changes fastest.
The devices are a block of a 4x4x8 slice.
Arguments:
- hidden: bfloat16 [512, 2048], P('dp'), parts along dimension 0
- lengths: int32 [512], P('dp'), parts along dimension 0
- k_cache: bfloat16 [2, 512, 512, 8, 64], P(None, 'dp', None, 'tp'), parts along dimension 1
- v_cache: bfloat16 [2, 512, 512, 8, 64], P(None, 'dp', None, 'tp'), parts along dimension 1
- attn_norm: bfloat16 [2, 2048], replicated
- w_qkv: bfloat16 [2, 2048, 8, 384], P(None, None, 'tp')
- w_out: bfloat16 [2, 2048, 2048], P(None, 'tp')
- mlp_norm: bfloat16 [2, 2048], replicated
- w_gate: bfloat16 [2, 2048, 8192], P(None, None, 'tp')
- w_up: bfloat16 [2, 2048, 8192], P(None, None, 'tp')
- w_down: bfloat16 [2, 8192, 2048], P(None, 'tp')
Outputs:
- output: bfloat16 [512, 2048], P('dp'), parts along dimension 0
There are 4 independent parts. A program takes and returns all parts, laid end to end along the dimension named above; an argument that names none is the same for every part.
All inputs are finite; a program needn't handle non-finite values.
Results may differ from a plain program's by a relative error of at most 0.0186567.
Values are sent between devices in bfloat16 or wider.
A program may use at most 768 MiB of HBM per device.

v0:
```python
import jax
import jax.numpy as jnp
from jax import lax
from jax.sharding import PartitionSpec as P

ROPE_BASE = 10000.0
NORM_EPS = 1e-5


def rms_norm(values, gain):
    wide = values.astype(jnp.float32)
    scale = lax.rsqrt(jnp.mean(wide * wide, axis=-1, keepdims=True) + NORM_EPS)
    return (wide * scale * gain.astype(jnp.float32)).astype(jnp.bfloat16)


def rotate(values, cosine, sine):
    half = values.shape[-1] // 2
    first = values[..., :half]
    second = values[..., half:]
    return jnp.concatenate([first * cosine - second * sine, second * cosine + first * sine], axis=-1)


def rope_tables(lengths, head_dim):
    inv_freq = ROPE_BASE ** (-jnp.arange(0, head_dim, 2, dtype=jnp.float32) / head_dim)
    angles = lengths.astype(jnp.float32)[:, None] * inv_freq[None, :]
    return jnp.cos(angles), jnp.sin(angles)


def attention(fused, keys_layer, values_layer, live, cosine, sine):
    group = fused.shape[2] - 2
    scale = fused.shape[3] ** -0.5
    wide = fused.astype(jnp.float32)
    query = rotate(wide[:, :, :group], cosine[:, None, None, :], sine[:, None, None, :]).astype(jnp.bfloat16)
    key_new = rotate(wide[:, :, group], cosine[:, None, :], sine[:, None, :]).astype(jnp.bfloat16)
    val_new = fused[:, :, group + 1]
    logits = jnp.einsum('bkgd,bskd->bkgs', query, keys_layer, preferred_element_type=jnp.float32) * scale
    logits = jnp.where(live[:, None, None, :], logits, -1e30)
    self_logit = jnp.einsum('clhe,cle->clh', query, key_new, preferred_element_type=jnp.float32) * scale
    peak = jnp.maximum(jnp.max(logits, axis=-1), self_logit)
    weights = jnp.exp(logits - peak[..., None]).astype(jnp.bfloat16)
    self_weight = jnp.exp(self_logit - peak).astype(jnp.bfloat16).astype(jnp.float32)
    denominator = jnp.sum(weights, axis=-1, dtype=jnp.float32) + self_weight
    numerator = jnp.einsum('bkgs,bskd->bkgd', weights, values_layer, preferred_element_type=jnp.float32)
    numerator = numerator + self_weight[..., None] * val_new.astype(jnp.float32)[:, :, None, :]
    return (numerator / denominator[..., None]).astype(jnp.bfloat16)


def solution(mesh):
    group_devs = mesh.shape['tp']

    def reduce_add(partial, residual):
        rows, d_model = partial.shape
        width = d_model // group_devs
        pieces = lax.all_to_all(partial.reshape(rows, group_devs, width), 'tp', 1, 1, tiled=True)
        own_part = lax.dynamic_slice_in_dim(residual, lax.axis_index('tp') * width, width, axis=1)
        summed = (own_part.astype(jnp.float32) + jnp.sum(pieces, axis=1, dtype=jnp.float32)).astype(jnp.bfloat16)
        return lax.all_gather(summed, 'tp', axis=1, tiled=True)

    def local_step(hidden, lengths, k_cache, v_cache, attn_norm, w_qkv, w_out, mlp_norm, w_gate, w_up, w_down):
        rows = hidden.shape[0]
        head_dim = k_cache.shape[4]
        cosine, sine = rope_tables(lengths, head_dim)
        live = jnp.arange(k_cache.shape[2])[None, :] < lengths[:, None]
        residual = hidden
        for layer in range(w_qkv.shape[0]):
            normed = rms_norm(residual, attn_norm[layer])
            fused = jnp.einsum('bd,dkf->bkf', normed, w_qkv[layer], preferred_element_type=jnp.float32).astype(jnp.bfloat16)
            fused = fused.reshape(rows, fused.shape[1], -1, head_dim)
            attended = attention(fused, k_cache[layer], v_cache[layer], live, cosine, sine)
            partial = jnp.dot(attended.reshape(rows, -1), w_out[layer], preferred_element_type=jnp.float32).astype(jnp.bfloat16)
            residual = reduce_add(partial, residual)
            normed = rms_norm(residual, mlp_norm[layer])
            gate_proj = jnp.dot(normed, w_gate[layer], preferred_element_type=jnp.float32).astype(jnp.bfloat16)
            up_proj = jnp.dot(normed, w_up[layer], preferred_element_type=jnp.float32).astype(jnp.bfloat16)
            activated = (jax.nn.silu(gate_proj.astype(jnp.float32)) * up_proj.astype(jnp.float32)).astype(jnp.bfloat16)
            partial = jnp.dot(activated, w_down[layer], preferred_element_type=jnp.float32).astype(jnp.bfloat16)
            residual = reduce_add(partial, residual)
        return residual

    cache_spec = P(None, 'dp', None, 'tp', None)
    in_specs = (P('dp', None), P('dp'), cache_spec, cache_spec, P(), P(None, None, 'tp', None),
                P(None, 'tp', None), P(), P(None, None, 'tp'), P(None, None, 'tp'), P(None, 'tp', None))
    return jax.shard_map(local_step, mesh=mesh, in_specs=in_specs, out_specs=P('dp', None), check_vma=False)
```

profile of v0, /device:TPU:81, one launch (start us, length us, event | category | flops | bytes accessed | tf_op | source)
XLA Modules:
  0.0 161.6 jit_solution(2831435366138425861)
XLA Ops:
  1.4 1.2 fusion.82
  2.7 0.8 slice_convert_fusion.1
  3.5 2.1 %fusion.74 = bf16[128,384]{1,0:T(8,128)(2,1)S(1)} fusion(bf16[2,2048,1,384]{3,1,2,0:T(8,128)(2,1)} %param.16, bf16[128,2048]{1,0:T(8,128)(2,1)} %param.11, f32[2048]{0:T(1024)S(1)} %bitcast.198, f32[128]{0:T(128)S(1)} %add_rsqrt_fusion.3), kind=kOutput, calls=%fused_computation.60 | convolution fusion | flops 202424320 | bytes 2204160 | tf_op jit(solution)/shard_map/bd,dkf->bkf/dot_general | solution.py:67
  6.7 4.7 %fusion.164 = (f32[128,4]{1,0:T(8,128)S(1)}, f32[128,4,512]{2,1,0:T(4,128)S(1)}) fusion(bf16[128,4,64]{2,1,0:T(4,128)(2,1)S(1)} %copy.65, bf16[2,128,512,1,64]{2,4,1,3,0:T(8,128)(2,1)} %bitcast.199, pred[128,512]{1,0:T(8,128)(4,1)S(1)} %iota_compare_fusion), kind=kOutput, calls=%fused_computation.178 | convolution fusion | flops 34340352 | bytes 9570304 | tf_op jit(solution)/shard_map/bkgd,bskd->bkgs/dot_general | solution.py:36
  12.2 5.8 %fusion.101 = bf16[128,4,64]{2,1,0:T(4,128)(2,1)S(1)} fusion(bf16[2,128,512,1,64]{2,4,1,3,0:T(8,128)(2,1)} %bitcast.201, f32[128,4]{1,0:T(8,128)S(1)} %get-tuple-element.7, f32[128,64]{1,0:T(8,128)S(1)} %copy.67, f32[128,4]{1,0:T(8,128)S(1)} %get-tuple-element.8, f32[128,4,512]{2,1,0:T(4,128)S(1)} %get-tuple-element.24, f32[128,4]{1,0:T(8,128)S(1)} %multiply_maximum_fusion.1), kind=kOutput, calls=%fused_computation.91 | convolution fusion | flops 34209792 | bytes 9541632 | tf_op jit(solution)/shard_map/bkgs,bskd->bkgd/dot_general | solution.py:43
  18.5 0.8 copy.94
  19.3 6.0 %all-to-all-start = ((bf16[128,8,256]{2,0,1:T(8,128)(2,1)}), bf16[128,8,256]{2,0,1:T(8,128)(2,1)S(1)}, u32[]{:S(2)}, u32[]{:S(2)}) async-start(bf16[128,8,256]{2,0,1:T(8,128)(2,1)} %bitcast.175), calls=%async_computation | async-start | bytes 1048576 | tf_op jit(solution)/shard_map/all_to_all | solution.py:54
  25.3 9.1 %all-to-all-done = bf16[128,8,256]{2,0,1:T(8,128)(2,1)S(1)} async-done(((bf16[128,8,256]{2,0,1:T(8,128)(2,1)}), bf16[128,8,256]{2,0,1:T(8,128)(2,1)S(1)}, u32[]{:S(2)}, u32[]{:S(2)}) %all-to-all-start) | async-done | bytes 524320 | tf_op jit(solution)/shard_map/all_to_all | solution.py:54
  34.5 0.9 add_convert_fusion.3
  35.4 14.2 %all_gather.12 = bf16[128,2048]{1,0:T(8,128)(2,1)S(1)} all-gather(bf16[128,256]{1,0:T(8,128)(2,1)S(1)} %add_convert_fusion.3), channel_id=1, replica_groups=mesh['dp'=4,'tp'=8] {'tp'}, dimensions={1}, use_global_device_ids=true | all-gather | bytes 589824 | tf_op jit(solution)/shard_map/all_gather | solution.py:57
  49.8 3.8 %fusion.39 = f32[128,1024]{1,0:T(8,128)} fusion(bf16[2,2048,1024]{2,1,0:T(8,128)(2,1)} %param.19, bf16[128,2048]{1,0:T(8,128)(2,1)S(1)} %all_gather.12, f32[2048]{0:T(1024)S(1)} %bitcast.196, f32[128]{0:T(128)S(1)} %add_rsqrt_fusion.2), kind=kOutput, calls=%fused_computation.47 | convolution fusion | flops 538181632 | bytes 5251584 | tf_op jit(solution)/shard_map/dot_general | solution.py:73
  53.6 5.1 %fusion.22 = bf16[128,2048]{1,0:T(8,128)(2,1)S(1)} fusion(bf16[2,1024,2048]{2,1,0:T(8,128)(2,1)} %param.21, bf16[2,2048,1024]{2,1,0:T(8,128)(2,1)} %param.20, f32[128,1024]{1,0:T(8,128)} %fusion.39, bf16[128,2048]{1,0:T(8,128)(2,1)S(1)} %all_gather.12, f32[2048]{0:T(1024)S(1)} %bitcast.197, f32[128]{0:T(128)S(1)} %add_rsqrt_fusion.2), kind=kOutput, calls=%fused_computation.26 | convolution fusion | flops 1076101120 | bytes 9970176 | tf_op jit(solution)/shard_map/dot_general | solution.py:76
  58.7 12.0 %all_to_all.20 = bf16[128,8,256]{2,0,1:T(8,128)(2,1)S(1)} all-to-all(bf16[128,8,256]{2,0,1:T(8,128)(2,1)S(1)} %bitcast.178), channel_id=1, replica_groups=mesh['dp'=4,'tp'=8] {'tp'}, dimensions={1} | all-to-all | bytes 1048576 | tf_op jit(solution)/shard_map/all_to_all | solution.py:54
  70.8 14.4 %all_gather.13 = bf16[128,2048]{1,0:T(8,128)(2,1)S(1)} all-gather(bf16[128,256]{1,0:T(8,128)(2,1)S(1)} %add_convert_fusion.2), channel_id=1, replica_groups=mesh['dp'=4,'tp'=8] {'tp'}, dimensions={1}, use_global_device_ids=true | all-gather | bytes 589824 | tf_op jit(solution)/shard_map/all_gather | solution.py:57
  85.4 1.9 %fusion.77 = bf16[128,384]{1,0:T(8,128)(2,1)S(1)} fusion(bf16[2,2048,1,384]{3,1,2,0:T(8,128)(2,1)} %param.16, bf16[128,2048]{1,0:T(8,128)(2,1)S(1)} %all_gather.13, f32[2048]{0:T(1024)S(1)} %bitcast.193, f32[128]{0:T(128)S(1)} %add_rsqrt_fusion.1), kind=kOutput, calls=%fused_computation.61 | convolution fusion | flops 202424320 | bytes 2204160 | tf_op jit(solution)/shard_map/bd,dkf->bkf/dot_general | solution.py:67
  88.1 4.7 %fusion.165 = (f32[128,4]{1,0:T(8,128)S(1)}, f32[128,4,512]{2,1,0:T(4,128)S(1)}) fusion(bf16[128,4,64]{2,1,0:T(4,128)(2,1)S(1)} %copy.73, bf16[2,128,512,1,64]{2,4,1,3,0:T(8,128)(2,1)} %bitcast.200, pred[128,512]{1,0:T(8,128)(4,1)S(1)} %iota_compare_fusion), kind=kOutput, calls=%fused_computation.179 | convolution fusion | flops 34340352 | bytes 9570304 | tf_op jit(solution)/shard_map/bkgd,bskd->bkgs/dot_general | solution.py:36
  93.8 5.8 %fusion.99 = bf16[128,4,64]{2,1,0:T(4,128)(2,1)S(1)} fusion(bf16[2,128,512,1,64]{2,4,1,3,0:T(8,128)(2,1)} %bitcast.202, f32[128,4]{1,0:T(8,128)S(1)} %get-tuple-element.5, f32[128,64]{1,0:T(8,128)S(1)} %copy.75, f32[128,4]{1,0:T(8,128)S(1)} %get-tuple-element.6, f32[128,4,512]{2,1,0:T(4,128)S(1)} %get-tuple-element.26, f32[128,4]{1,0:T(8,128)S(1)} %multiply_maximum_fusion), kind=kOutput, calls=%fused_computation.89 | convolution fusion | flops 34209792 | bytes 9541632 | tf_op jit(solution)/shard_map/bkgs,bskd->bkgd/dot_general | solution.py:43
  100.1 12.0 %all_to_all.21 = bf16[128,8,256]{2,0,1:T(8,128)(2,1)S(1)} all-to-all(bf16[128,8,256]{2,0,1:T(8,128)(2,1)S(1)} %bitcast.179), channel_id=1, replica_groups=mesh['dp'=4,'tp'=8] {'tp'}, dimensions={1} | all-to-all | bytes 1048576 | tf_op jit(solution)/shard_map/all_to_all | solution.py:54
  112.2 14.2 %all_gather.14 = bf16[128,2048]{1,0:T(8,128)(2,1)S(1)} all-gather(bf16[128,256]{1,0:T(8,128)(2,1)S(1)} %add_convert_fusion.1), channel_id=1, replica_groups=mesh['dp'=4,'tp'=8] {'tp'}, dimensions={1}, use_global_device_ids=true | all-gather | bytes 589824 | tf_op jit(solution)/shard_map/all_gather | solution.py:57
  126.6 2.9 %fusion.57 = f32[128,1024]{1,0:T(8,128)S(1)} fusion(bf16[2,2048,1024]{2,1,0:T(8,128)(2,1)} %param.19, bf16[128,2048]{1,0:T(8,128)(2,1)S(1)} %all_gather.14, f32[2048]{0:T(1024)S(1)} %bitcast.194, f32[128]{0:T(128)S(1)} %add_rsqrt_fusion), kind=kOutput, calls=%fused_computation.53 | convolution fusion | flops 538181632 | bytes 5251584 | tf_op jit(solution)/shard_map/dot_general | solution.py:73
  129.6 4.9 %fusion.25 = bf16[128,2048]{1,0:T(8,128)(2,1)S(1)} fusion(bf16[2,1024,2048]{2,1,0:T(8,128)(2,1)} %param.21, bf16[2,2048,1024]{2,1,0:T(8,128)(2,1)} %param.20, f32[128,1024]{1,0:T(8,128)S(1)} %fusion.57, bf16[128,2048]{1,0:T(8,128)(2,1)S(1)} %all_gather.14, f32[2048]{0:T(1024)S(1)} %bitcast.195, f32[128]{0:T(128)S(1)} %add_rsqrt_fusion), kind=kOutput, calls=%fused_computation.27 | convolution fusion | flops 1076101120 | bytes 9970176 | tf_op jit(solution)/shard_map/dot_general | solution.py:76
  134.5 12.0 %all_to_all.22 = bf16[128,8,256]{2,0,1:T(8,128)(2,1)S(1)} all-to-all(bf16[128,8,256]{2,0,1:T(8,128)(2,1)S(1)} %bitcast.180), channel_id=1, replica_groups=mesh['dp'=4,'tp'=8] {'tp'}, dimensions={1} | all-to-all | bytes 1048576 | tf_op jit(solution)/shard_map/all_to_all | solution.py:54
  146.6 14.2 %all_gather.15 = bf16[128,2048]{1,0:T(8,128)(2,1)S(1)} all-gather(bf16[128,256]{1,0:T(8,128)(2,1)S(1)} %add_convert_fusion), channel_id=1, replica_groups=mesh['dp'=4,'tp'=8] {'tp'}, dimensions={1}, use_global_device_ids=true | all-gather | bytes 589824 | tf_op jit(solution)/shard_map/all_gather | solution.py:57
  160.8 0.8 copy.96
  (60 shorter events, 6.9 us)
Async XLA Ops:
  11.5 6.6 %copy-start = (bf16[2,256,2048]{2,1,0:T(8,128)(2,1)S(1)}, bf16[2,256,2048]{2,1,0:T(8,128)(2,1)}, u32[]{:S(2)}) copy-start(bf16[2,256,2048]{2,1,0:T(8,128)(2,1)} %param.17) | copy-start | bytes 6291460
  12.2 13.1 %copy-start.1 = (bf16[2,2048]{1,0:T(2,128)(2,1)S(1)}, bf16[2,2048]{1,0:T(2,128)(2,1)}, u32[]{:S(2)}) copy-start(bf16[2,2048]{1,0:T(2,128)(2,1)} %param.18) | copy-start | bytes 24580
  19.3 15.2 %all-to-all-start = ((bf16[128,8,256]{2,0,1:T(8,128)(2,1)}), bf16[128,8,256]{2,0,1:T(8,128)(2,1)S(1)}, u32[]{:S(2)}, u32[]{:S(2)}) async-start(bf16[128,8,256]{2,0,1:T(8,128)(2,1)} %bitcast.175), calls=%async_computation | async-start | bytes 1048576 | tf_op jit(solution)/shard_map/all_to_all | solution.py:54
where the time goes:
time: 162 us
  blocking collectives  93 us (57%)
  matrix products  42.9 us (26%)
  waiting for transfers between devices  9.12 us (6%)
  other arithmetic  7.23 us (4%)
  starting transfers between devices  6.02 us (4%)
  local copies, waits for them, and re-layouts  2.96 us (2%)
    all_gather x4, blocking collectives, reduce_add(): return lax.all_gather(summed, 'tp', axis=1, tiled=True)  57 us
    all_to_all x3, blocking collectives, reduce_add(): lax.all_to_all(partial.reshape(rows, group_devs, width), 'tp', 1, 1, tile...  36.1 us
    dot_general x2, matrix products, attention(): jnp.einsum('bkgs,bskd->bkgd', weights, values_layer, preferred_element_ty...  11.5 us
    dot_general x2, matrix products, local_step(): jnp.dot(activated, w_down[layer], preferred_element_type=jnp.float32)  9.95 us
    dot_general x2, matrix products, attention(): jnp.einsum('bkgd,bskd->bkgs', query, keys_layer, preferred_element_type=j...  9.47 us
    all_to_all x1, waiting for transfers between devices, reduce_add(): lax.all_to_all(partial.reshape(rows, group_devs, width), 'tp', 1, 1, tile...  9.12 us
    dot_general x2, matrix products, local_step(): jnp.dot(normed, w_gate[layer], preferred_element_type=jnp.float32)  6.71 us
    all_to_all x1, starting transfers between devices, reduce_add(): lax.all_to_all(partial.reshape(rows, group_devs, width), 'tp', 1, 1, tile...  6.02 us
  transfers between devices with their start and end apart: 1, of which 1 were waited for; matrix products, arithmetic and copies ran while one was open for 0% of the time, Pallas kernels for 0%

commit v1 on v0

v1 whole, which is shorter than its diff:
```python
import functools
import math

import jax
import jax.numpy as jnp
from jax import lax
from jax.experimental import pallas as pl
from jax.experimental.pallas import tpu as pltpu
from jax.sharding import PartitionSpec as P

ROPE_BASE = 10000.0
NORM_EPS = 1e-5
NEG = -1e30
TILE_ROWS = 16
F32 = jnp.float32
BF16 = jnp.bfloat16


def dot(a, b):
    return jnp.dot(a, b, preferred_element_type=F32)


class Comm:
    def __init__(self, send, recv):
        self.send, self.recv = send, recv
        self.sent, self.base, self.open = 0, 0, []

    def start(self, slot, src, dst, device):
        copy = pltpu.make_async_remote_copy(
            src_ref=src, dst_ref=dst, send_sem=self.send.at[self.sent], recv_sem=self.recv.at[self.base + slot],
            device_id={"tp": device}, device_id_type=pl.DeviceIdType.MESH)
        copy.start()
        self.sent += 1
        self.open.append(copy)

    def wait(self, slot, ref):
        pltpu.make_async_remote_copy(
            src_ref=ref, dst_ref=ref, send_sem=self.send.at[0], recv_sem=self.recv.at[self.base + slot],
            device_id={"tp": lax.axis_index("tp")}, device_id_type=pl.DeviceIdType.MESH).wait_recv()

    def drain(self):
        for copy in self.open:
            copy.wait_send()
        self.open = []


def kernel(group, layers,
           hidden, lengths, k_hbm, v_hbm, attn_norm, w_qkv, w_out, mlp_norm, w_gate, w_up, w_down, out,
           x_in, len_in, gains, wq, wo, wg, wu, wd, kbuf, vbuf,
           cos_tab, sin_tab, len_tab, qq, kz, vz, attn, normed, act,
           part, far_in, sib_in, own_in, near_in, rel_out, rel_in, xg,
           load_sem, k_sem, v_sem, send_sem, recv_sem):
    rows, d_model = hidden.shape
    half = rows // 2
    width = d_model // group
    chips = group // 2
    me = lax.axis_index("tp")
    chip, core = me // 2, me % 2
    sibling = chip * 2 + (1 - core)
    right, left, far = (chip + 1) % chips, (chip + chips - 1) % chips, (chip + 2) % chips
    n_tiles = rows // TILE_ROWS
    seq = kbuf.shape[2]
    head_dim = kbuf.shape[1]
    comm = Comm(send_sem, recv_sem)

    loads = []

    def load(src, dst):
        copy = pltpu.make_async_copy(src, dst, load_sem.at[len(loads)])
        copy.start()
        loads.append(copy)
        return copy

    def load_cache(layer):
        for i in range(n_tiles):
            rng = pl.ds(i * TILE_ROWS, TILE_ROWS)
            pltpu.make_async_copy(k_hbm.at[layer, rng], kbuf.at[rng], k_sem.at[i]).start()
            pltpu.make_async_copy(v_hbm.at[layer, rng], vbuf.at[rng], v_sem.at[i]).start()

    ld_len = load(lengths, len_in)
    ld_x = load(hidden, x_in)
    ld_gain = [load(attn_norm, gains.at[0]), load(mlp_norm, gains.at[1])]
    ld_q = [load(w_qkv.at[0], wq.at[0])]
    load_cache(0)
    ld_o = [load(w_out.at[0], wo.at[0])]
    ld_g, ld_u, ld_d = [], [], []

    barrier = pltpu.get_barrier_semaphore()
    for peer in (sibling, right * 2, right * 2 + 1, left * 2, left * 2 + 1):
        pl.semaphore_signal(barrier, inc=1, device_id={"tp": peer}, device_id_type=pl.DeviceIdType.MESH)
    pl.semaphore_wait(barrier, 5)

    ld_len.wait()
    len_row = jnp.broadcast_to(len_in[...].astype(F32), (rows, rows))
    len_tab[...] = len_row.T
    freq = lax.broadcasted_iota(jnp.int32, (head_dim // 2, rows), 0).astype(F32)
    angles = len_row[:head_dim // 2] * jnp.exp(freq * (-2.0 / head_dim * math.log(ROPE_BASE)))
    cosine, sine = jnp.cos(angles), jnp.sin(angles)
    cos_tab[...] = jnp.concatenate([cosine] * 4, axis=0).T
    sin_tab[...] = jnp.concatenate([-sine, sine, -sine, sine], axis=0).T

    def rms_norm(pieces, gain_row):
        total = jnp.zeros((rows, 1), F32)
        for i in range(group):
            wide = pieces(i)
            total = total + jnp.sum(wide * wide, axis=1, keepdims=True)
        scale = lax.rsqrt(total / d_model + NORM_EPS)
        for i in range(group):
            cols = slice(i * width, (i + 1) * width)
            normed[:, cols] = (pieces(i) * scale * gain_row(cols)).astype(BF16)

    def attention(layer):
        fused = dot(normed[...], wq[layer]).astype(BF16).astype(F32)
        lane = lax.broadcasted_iota(jnp.int32, (rows, 128), 1)
        first = lane % head_dim < head_dim // 2
        low = lane < head_dim
        cos, sin = cos_tab[...], sin_tab[...]

        def rope(x):
            swapped = jnp.where(first, pltpu.roll(x, 128 - head_dim // 2, 1), pltpu.roll(x, head_dim // 2, 1))
            return (x * cos + swapped * sin).astype(BF16).astype(F32)

        for pair in range(2):
            x = rope(fused[:, pair * 128:(pair + 1) * 128])
            swap = pltpu.roll(x, head_dim, 1)
            qq[2 * pair] = jnp.where(low, x, swap)
            qq[2 * pair + 1] = jnp.where(low, swap, x)
        kv = fused[:, 256:384]
        kz[...] = jnp.where(low, rope(kv), 0.0)
        vz[...] = pltpu.roll(kv, head_dim, 1)

        row16 = lax.broadcasted_iota(jnp.int32, (TILE_ROWS, 128), 0)
        high16 = lax.broadcasted_iota(jnp.int32, (TILE_ROWS, 128), 1) // head_dim
        pos = lax.broadcasted_iota(jnp.int32, (TILE_ROWS, seq), 1).astype(F32)
        col_row = lax.broadcasted_iota(jnp.int32, (head_dim, 4 * TILE_ROWS), 1) % TILE_ROWS

        def tile(i):
            rng = pl.ds(pl.multiple_of(i * TILE_ROWS, TILE_ROWS), TILE_ROWS)
            queries = [qq[g, rng, :] for g in range(4)]
            lhs = jnp.concatenate([
                jnp.concatenate([jnp.where(row16 == 2 * j + high16, q, 0.0).astype(BF16) for j in range(TILE_ROWS // 2)], axis=1)
                for q in queries], axis=0)
            pltpu.make_async_copy(k_hbm.at[layer, rng], kbuf.at[rng], k_sem.at[i]).wait()
            logits = dot(lhs, kbuf[rng].reshape(TILE_ROWS * head_dim, seq)) * head_dim ** -0.5
            live = pos < jnp.concatenate([len_tab[rng, :]] * (seq // 128), axis=1)
            keys = kz[rng, :]
            peaks, weights, sums, selfs = [], [], [], []
            for g in range(4):
                s = jnp.where(live, logits[g * TILE_ROWS:(g + 1) * TILE_ROWS], NEG)
                own = jnp.sum(queries[g] * keys, axis=1, keepdims=True) * head_dim ** -0.5
                peak = jnp.maximum(jnp.max(s, axis=1, keepdims=True), own)
                w = jnp.exp(s - peak).astype(BF16)
                w_own = jnp.exp(own - peak).astype(BF16).astype(F32)
                weights.append(w)
                selfs.append(w_own)
                sums.append(jnp.sum(w.astype(F32), axis=1, keepdims=True) + w_own)
            w_all = jnp.concatenate(weights, axis=0)
            pltpu.make_async_copy(v_hbm.at[layer, rng], vbuf.at[rng], v_sem.at[i]).wait()
            picked = lax.dot_general(vbuf[rng].reshape(TILE_ROWS * head_dim, seq), w_all, (((1,), (1,)), ((), ())),
                                     preferred_element_type=F32)
            numer = jnp.zeros((head_dim, 4 * TILE_ROWS), F32)
            for b in range(TILE_ROWS):
                numer = jnp.where(col_row == b, picked[b * head_dim:(b + 1) * head_dim], numer)
            numer = numer.T
            values = vz[rng, :][:, :head_dim]
            heads = [((numer[g * TILE_ROWS:(g + 1) * TILE_ROWS] + selfs[g] * values) / sums[g]).astype(BF16)
                     for g in range(4)]
            attn[rng, :] = jnp.concatenate(heads, axis=1)

        def body(i, carry):
            tile(2 * i)
            tile(2 * i + 1)
            return carry

        lax.fori_loop(0, n_tiles // 2, body, 0)

    def reduce_add(r, lhs, weight, own_rows):
        comm.base = r * SLOTS
        p, x = part.at[r], xg.at[r]
        top, bottom = pl.ds(0, half), pl.ds(half, half)

        def produce(index, target):
            cols = pl.ds(pl.multiple_of(target * 2 * width, 128), 2 * width)
            block = dot(lhs, weight[:, cols]).astype(BF16)
            p[index, 0] = block[:, :width]
            p[index, 1] = block[:, width:]

        produce(0, far)
        for k in range(2):
            comm.start(core, p.at[0, k, top], far_in.at[r, 0, core], right * 2 + k)
            comm.start(2 + core, p.at[0, k, bottom], far_in.at[r, 1, core], left * 2 + k)
        produce(1, right)
        comm.start(4, p.at[1, 1 - core, top], sib_in.at[r, 0], sibling)
        for k in range(2):
            comm.start(7 + core, p.at[1, k, bottom], near_in.at[r, 0, core], right * 2 + k)
        produce(2, left)
        comm.start(5, p.at[2, 1 - core, bottom], sib_in.at[r, 1], sibling)
        for k in range(2):
            comm.start(9 + core, p.at[2, k, top], near_in.at[r, 1, core], left * 2 + k)
        produce(3, chip)
        comm.start(6, p.at[3, 1 - core], own_in.at[r], sibling)

        for way, rng, target in ((0, top, right), (1, bottom, left)):
            for k in range(2):
                comm.wait(2 * way + k, far_in.at[r, way, k])
            comm.wait(4 + way, sib_in.at[r, way])
            rel_out[r, way] = (far_in[r, way, 0].astype(F32) + far_in[r, way, 1].astype(F32)
                               + p[1 + way, core, rng].astype(F32) + sib_in[r, way].astype(F32))
            comm.start(11 + way, rel_out.at[r, way], rel_in.at[r, way], target * 2 + core)

        comm.wait(6, own_in.at[r])
        mine = {}
        for rng in (top, bottom):
            mine[rng.start] = (own_rows(rng).astype(F32) + p[3, core, rng].astype(F32)
                               + own_in[r, rng].astype(F32))
        to_right, to_left = right * 2 + core, left * 2 + core
        for way, rng, slot, target in ((0, top, 13, to_right), (1, bottom, 14, to_left)):
            for k in range(2):
                comm.wait(7 + 2 * (1 - way) + k, near_in.at[r, 1 - way, k])
            comm.wait(11 + way, rel_in.at[r, way])
            total = (mine[rng.start] + near_in[r, 1 - way, 0].astype(F32) + near_in[r, 1 - way, 1].astype(F32)
                     + rel_in[r, way])
            x[me, rng] = total.astype(BF16)
            comm.start(slot, x.at[me, rng], x.at[me, rng], target)
        comm.start(15, x.at[me, top], x.at[me, top], to_left)
        comm.start(16, x.at[me, bottom], x.at[me, bottom], to_right)
        comm.start(19, x.at[me], x.at[me], sibling)
        from_left, from_right, from_far = left * 2 + core, right * 2 + core, far * 2 + core
        for slot, origin, rng, onward, target in (
                (13, from_left, top, 17, to_right), (14, from_right, bottom, 18, to_left),
                (15, from_right, top, None, None), (16, from_left, bottom, None, None),
                (17, from_far, top, None, None), (18, from_far, bottom, None, None)):
            piece = x.at[origin, rng]
            comm.wait(slot, piece)
            if onward is not None:
                comm.start(onward, piece, piece, target)
            comm.start(slot + 7, piece, piece, sibling)
        other = 1 - core
        comm.wait(19, x.at[sibling])
        for slot, origin, rng in ((20, left, top), (21, right, bottom), (22, right, top), (23, left, bottom),
                                  (24, far, top), (25, far, bottom)):
            comm.wait(slot, x.at[origin * 2 + other, rng])

    for layer in range(layers):
        if layer == 0:
            ld_x.wait()
            for copy in ld_gain:
                copy.wait()

        def gain(which):
            return lambda cols: gains[which, layer:layer + 1, cols].astype(F32)

        first = 2 * layer
        if layer == 0:
            rms_norm(lambda i: x_in[:, i * width:(i + 1) * width].astype(F32), gain(0))
            own_cols = pl.ds(pl.multiple_of(me * width, 128), width)
            own_rows = lambda rng: x_in[rng, own_cols]
        else:
            rms_norm(lambda i: xg[first - 1, i].astype(F32), gain(0))
            own_rows = lambda rng: xg[first - 1, me, rng]
        ld_q[layer].wait()
        attention(layer)
        if layer == 0:
            for at in range(layers):
                ld_g.append(load(w_gate.at[at], wg.at[at]))
                ld_u.append(load(w_up.at[at], wu.at[at]))
                ld_d.append(load(w_down.at[at], wd.at[at]))
                if at + 1 < layers:
                    ld_q.append(load(w_qkv.at[at + 1], wq.at[at + 1]))
                    load_cache(at + 1)
                    ld_o.append(load(w_out.at[at + 1], wo.at[at + 1]))
        ld_o[layer].wait()
        reduce_add(first, attn[...], wo.at[layer], own_rows)
        rms_norm(lambda i: xg[first, i].astype(F32), gain(1))
        ld_g[layer].wait()
        ld_u[layer].wait()
        n = normed[...]
        for c in range(0, act.shape[1], 256):
            g = dot(n, wg[layer, :, c:c + 256]).astype(BF16).astype(F32)
            u = dot(n, wu[layer, :, c:c + 256]).astype(BF16).astype(F32)
            act[:, c:c + 256] = (g * jax.nn.sigmoid(g) * u).astype(BF16)
        ld_d[layer].wait()
        reduce_add(first + 1, act[...], wd.at[layer], lambda rng: xg[first, me, rng])
    for i in range(group):
        out[:, i * width:(i + 1) * width] = xg[2 * layers - 1, i]
    comm.drain()


SLOTS = 26


def solution(mesh):
    group = mesh.shape["tp"]

    def local_step(hidden, lengths, k_cache, v_cache, attn_norm, w_qkv, w_out, mlp_norm, w_gate, w_up, w_down):
        rows, d_model = hidden.shape
        layers, _, seq, _, head_dim = k_cache.shape
        width = d_model // group
        half = rows // 2
        rounds = 2 * layers
        fused_width = w_qkv.shape[-1]
        n_tiles = rows // TILE_ROWS
        keys = jnp.transpose(k_cache, (0, 1, 3, 4, 2)).reshape(layers, rows, head_dim, seq)
        values = jnp.transpose(v_cache, (0, 1, 3, 4, 2)).reshape(layers, rows, head_dim, seq)
        w_qkv = w_qkv.reshape(layers, d_model, fused_width)
        any_spec = pl.BlockSpec(memory_space=pl.ANY)
        sem = pltpu.SemaphoreType.DMA
        n_loads = 4 + 5 * layers
        return pl.pallas_call(
            functools.partial(kernel, group, layers),
            out_shape=jax.ShapeDtypeStruct((rows, d_model), BF16),
            in_specs=[any_spec] * 11,
            out_specs=pl.BlockSpec(memory_space=pltpu.VMEM),
            scratch_shapes=[
                pltpu.VMEM((rows, d_model), BF16),
                pltpu.VMEM((1, rows), jnp.int32),
                pltpu.VMEM((2, layers, d_model), BF16),
                pltpu.VMEM(w_qkv.shape, BF16),
                pltpu.VMEM(w_out.shape, BF16),
                pltpu.VMEM(w_gate.shape, BF16),
                pltpu.VMEM(w_up.shape, BF16),
                pltpu.VMEM(w_down.shape, BF16),
                pltpu.VMEM((rows, head_dim, seq), BF16),
                pltpu.VMEM((rows, head_dim, seq), BF16),
                pltpu.VMEM((rows, 128), F32),
                pltpu.VMEM((rows, 128), F32),
                pltpu.VMEM((rows, 128), F32),
                pltpu.VMEM((4, rows, 128), F32),
                pltpu.VMEM((rows, 128), F32),
                pltpu.VMEM((rows, 128), F32),
                pltpu.VMEM((rows, w_out.shape[1]), BF16),
                pltpu.VMEM((rows, d_model), BF16),
                pltpu.VMEM((rows, w_down.shape[1]), BF16),
                pltpu.VMEM((rounds, 4, 2, rows, width), BF16),
                pltpu.VMEM((rounds, 2, 2, half, width), BF16),
                pltpu.VMEM((rounds, 2, half, width), BF16),
                pltpu.VMEM((rounds, rows, width), BF16),
                pltpu.VMEM((rounds, 2, 2, half, width), BF16),
                pltpu.VMEM((rounds, 2, half, width), F32),
                pltpu.VMEM((rounds, 2, half, width), F32),
                pltpu.VMEM((rounds, group, rows, width), BF16),
                sem((n_loads,)),
                sem((n_tiles,)),
                sem((n_tiles,)),
                sem((rounds * SLOTS,)),
                sem((rounds * SLOTS,)),
            ],
            compiler_params=pltpu.CompilerParams(
                collective_id=0, has_side_effects=True, vmem_limit_bytes=63 * 1024 * 1024),
            cost_estimate=pl.CostEstimate(flops=4 * 10**9, bytes_accessed=64 * 10**6, transcendentals=10**6),
            name="decode_layers",
        )(hidden, lengths.reshape(1, rows), keys, values, attn_norm, w_qkv, w_out, mlp_norm, w_gate, w_up, w_down)

    cache_spec = P(None, "dp", None, "tp", None)
    in_specs = (P("dp", None), P("dp"), cache_spec, cache_spec, P(), P(None, None, "tp", None),
                P(None, "tp", None), P(), P(None, None, "tp"), P(None, None, "tp"), P(None, "tp", None))
    return jax.shard_map(local_step, mesh=mesh, in_specs=in_specs, out_specs=P("dp", None), check_vma=False)
```

time: 162 us -> 98.2 us (0.61)
  Pallas kernels: 0 us -> 96.2 us
  blocking collectives: 93 us -> 0 us
  matrix products: 42.9 us -> 0 us
  waiting for transfers between devices: 9.12 us -> 0 us
  other arithmetic: 7.23 us -> 0 us
  starting transfers between devices: 6.02 us -> 0 us
    pallas_call x0 -> x1, Pallas kernels: none -> 96.2 us  [local_step(): pl.pallas_call(functools.partial(kernel, group, layers), out_shape=jax.Sh...]
    all_gather x4 -> x0, blocking collectives: 57 us -> none  [reduce_add(): return lax.all_gather(summed, 'tp', axis=1, tiled=True)]
    dot_general x14 -> x0, matrix products: 42.9 us -> none  [the longest x2 11.5 us: attention(): jnp.einsum('bkgs,bskd->bkgd', weights, values_layer, preferred_element_ty...]
    all_to_all x3 -> x0, blocking collectives: 36.1 us -> none  [reduce_add(): lax.all_to_all(partial.reshape(rows, group_devs, width), 'tp', 1, 1, tile...]
    all_to_all x1 -> x0, waiting for transfers between devices: 9.12 us -> none  [reduce_add(): lax.all_to_all(partial.reshape(rows, group_devs, width), 'tp', 1, 1, tile...]
    all_to_all x1 -> x0, starting transfers between devices: 6.02 us -> none  [reduce_add(): lax.all_to_all(partial.reshape(rows, group_devs, width), 'tp', 1, 1, tile...]
    reduce_sum x10 -> x0, other arithmetic: 3.4 us -> none  [the longest x4 1.79 us: rms_norm(): scale = lax.rsqrt(jnp.mean(wide * wide, axis=-1, keepdims=True) + NORM_EPS)]
    convert_element_type x7 -> x0, other arithmetic: 1.64 us -> none  [the longest x4 0.94 us: reduce_add(): (own_part.astype(jnp.float32) + jnp.sum(pieces, axis=1, dtype=jnp.float32...]
  transfers between devices with their start and end apart: 1 -> 0, of which waited for: 1 -> 0; matrix products, arithmetic and copies ran while one was open for 0% -> 0% of each run, Pallas kernels for 0% -> 0%
where the time goes in v1:
time: 98.2 us; the launch traced here: 98.1 us
  Pallas kernels  96.2 us (98%)
  local copies, waits for them, and re-layouts  1.88 us (2%)
    pallas_call x1, Pallas kernels, local_step(): pl.pallas_call(functools.partial(kernel, group, layers), out_shape=jax.Sh...  96.2 us

profile of v1, /device:TPU:81, one launch (start us, length us, event | category | flops | bytes accessed | tf_op | source)
XLA Modules:
  0.0 98.1 jit_solution(9601023704376213886)
XLA Ops:
  0.0 96.2 %decode_layers.1 = bf16[128,2048]{1,0:T(8,128)(2,1)} custom-call(bf16[128,2048]{1,0:T(8,128)(2,1)} %hidden.1, s32[1,128]{1,0:T(1,128)} %bitcast.15, bf16[2,128,64,512]{3,2,1,0:T(8,128)(2,1)} %bitcast.12, bf16[2,128,64,512]{3,2,1,0:T(8,128)(2,1)} %bitcast.13, bf16[2,2048]{1,0:T(2,128)(2,1)} %attn_norm.1, bf16[2,2048,384]{2,1,0:T(8,128)(2,1)} %bitcast.14, ...), custom_call_target="tpu_custom_call" | custom-call | flops 4000000000 | bytes 64000000 | tf_op jit(solution)/shard_map/decode_layers/pallas_call | solution.py:309
  96.2 1.9 %copy.15 = bf16[128,2048]{1,0:T(8,128)(2,1)} copy(bf16[128,2048]{1,0:T(8,128)(2,1)} %decode_layers.1) | data formatting | bytes 1048576

commit v2 on v1

v2 whole, which is shorter than its diff:
```python
import functools
import math

import jax
import jax.numpy as jnp
from jax import lax
from jax.experimental import pallas as pl
from jax.experimental.pallas import tpu as pltpu
from jax.sharding import PartitionSpec as P

ROPE_BASE = 10000.0
NORM_EPS = 1e-5
NEG = -1e30
TILE_ROWS = 16
VMEM_MIB = 56
F32 = jnp.float32
BF16 = jnp.bfloat16


def dot(a, b):
    return jnp.dot(a, b, preferred_element_type=F32)


def remote(src, dst, send_sem, recv_sem, device):
    return pltpu.make_async_remote_copy(
        src_ref=src, dst_ref=dst, send_sem=send_sem, recv_sem=recv_sem,
        device_id={"tp": device}, device_id_type=pl.DeviceIdType.MESH)


def kernel(group, layers, parts,
           hidden, lengths, k_hbm, v_hbm, attn_norm, w_qkv, w_out, mlp_norm, w_gate, w_up, w_down, out,
           x_in, len_in, gains, wq, wo, wg, wu, wd, kbuf, vbuf,
           cos_tab, sin_tab, len_tab, qq, kz, vz, attn, normed, act,
           block_out, block_in, xg,
           load_sem, k_sem, v_sem, rs_send, rs_recv, ag_send, ag_recv):
    rows, d_model = hidden.shape
    size = rows // parts
    width = d_model // group
    chips = group // 2
    me = lax.axis_index("tp")
    chip, core = me // 2, me % 2
    other = 1 - core
    sibling = chip * 2 + other
    right, left, far = (chip + 1) % chips, (chip + chips - 1) % chips, (chip + 2) % chips
    n_tiles = rows // TILE_ROWS
    seq = kbuf.shape[2]
    head_dim = kbuf.shape[1]
    ranges = [pl.ds(p * size, size) for p in range(parts)]

    loads = []

    def load(src, dst):
        copy = pltpu.make_async_copy(src, dst, load_sem.at[len(loads)])
        copy.start()
        loads.append(copy)
        return copy

    def load_cache(layer):
        for i in range(n_tiles):
            rng = pl.ds(i * TILE_ROWS, TILE_ROWS)
            pltpu.make_async_copy(k_hbm.at[layer, rng], kbuf.at[rng], k_sem.at[i]).start()
            pltpu.make_async_copy(v_hbm.at[layer, rng], vbuf.at[rng], v_sem.at[i]).start()

    ld_len = load(lengths, len_in)
    ld_x = load(hidden, x_in)
    ld_gain = [load(attn_norm, gains.at[0]), load(mlp_norm, gains.at[1])]
    ld_q = [load(w_qkv.at[0], wq.at[0])]
    load_cache(0)
    ld_o = [load(w_out.at[0], wo.at[0])]
    ld_g, ld_u, ld_d = [], [], []

    barrier = pltpu.get_barrier_semaphore()
    for step in range(1, group):
        pl.semaphore_signal(barrier, inc=1, device_id={"tp": (me + step) % group}, device_id_type=pl.DeviceIdType.MESH)
    pl.semaphore_wait(barrier, group - 1)

    ld_len.wait()
    len_row = jnp.broadcast_to(len_in[...].astype(F32), (rows, rows))
    len_tab[...] = len_row.T
    freq = lax.broadcasted_iota(jnp.int32, (head_dim // 2, rows), 0).astype(F32)
    angles = len_row[:head_dim // 2] * jnp.exp(freq * (-2.0 / head_dim * math.log(ROPE_BASE)))
    cosine, sine = jnp.cos(angles), jnp.sin(angles)
    cos_tab[...] = jnp.concatenate([cosine] * 4, axis=0).T
    sin_tab[...] = jnp.concatenate([-sine, sine, -sine, sine], axis=0).T

    def rms_norm(p, pieces, gain_row):
        total = jnp.zeros((size, 1), F32)
        for i in range(group):
            wide = pieces(i)
            total = total + jnp.sum(wide * wide, axis=1, keepdims=True)
        scale = lax.rsqrt(total / d_model + NORM_EPS)
        for i in range(group):
            cols = slice(i * width, (i + 1) * width)
            normed[ranges[p], cols] = (pieces(i) * scale * gain_row(cols)).astype(BF16)

    def attention(p, layer):
        part = ranges[p]
        fused = dot(normed[part, :], wq[layer]).astype(BF16).astype(F32)
        lane = lax.broadcasted_iota(jnp.int32, (size, 128), 1)
        first = lane % head_dim < head_dim // 2
        low = lane < head_dim
        cos, sin = cos_tab[part, :], sin_tab[part, :]

        def rope(x):
            swapped = jnp.where(first, pltpu.roll(x, 128 - head_dim // 2, 1), pltpu.roll(x, head_dim // 2, 1))
            return (x * cos + swapped * sin).astype(BF16).astype(F32)

        for pair in range(2):
            x = rope(fused[:, pair * 128:(pair + 1) * 128])
            swap = pltpu.roll(x, head_dim, 1)
            qq[2 * pair, part] = jnp.where(low, x, swap)
            qq[2 * pair + 1, part] = jnp.where(low, swap, x)
        kv = fused[:, 256:384]
        kz[part, :] = jnp.where(low, rope(kv), 0.0)
        vz[part, :] = pltpu.roll(kv, head_dim, 1)

        row16 = lax.broadcasted_iota(jnp.int32, (TILE_ROWS, 128), 0)
        high16 = lax.broadcasted_iota(jnp.int32, (TILE_ROWS, 128), 1) // head_dim
        pos = lax.broadcasted_iota(jnp.int32, (TILE_ROWS, seq), 1).astype(F32)
        col_row = lax.broadcasted_iota(jnp.int32, (head_dim, 4 * TILE_ROWS), 1) % TILE_ROWS

        def tile(i):
            rng = pl.ds(pl.multiple_of(i * TILE_ROWS, TILE_ROWS), TILE_ROWS)
            queries = [qq[g, rng, :] for g in range(4)]
            lhs = jnp.concatenate([
                jnp.concatenate([jnp.where(row16 == 2 * j + high16, q, 0.0).astype(BF16) for j in range(TILE_ROWS // 2)], axis=1)
                for q in queries], axis=0)
            pltpu.make_async_copy(k_hbm.at[layer, rng], kbuf.at[rng], k_sem.at[i]).wait()
            logits = dot(lhs, kbuf[rng].reshape(TILE_ROWS * head_dim, seq)) * head_dim ** -0.5
            live = pos < jnp.concatenate([len_tab[rng, :]] * (seq // 128), axis=1)
            keys = kz[rng, :]
            weights, sums, selfs = [], [], []
            for g in range(4):
                s = jnp.where(live, logits[g * TILE_ROWS:(g + 1) * TILE_ROWS], NEG)
                own = jnp.sum(queries[g] * keys, axis=1, keepdims=True) * head_dim ** -0.5
                peak = jnp.maximum(jnp.max(s, axis=1, keepdims=True), own)
                w = jnp.exp(s - peak).astype(BF16)
                w_own = jnp.exp(own - peak).astype(BF16).astype(F32)
                weights.append(w)
                selfs.append(w_own)
                sums.append(jnp.sum(w.astype(F32), axis=1, keepdims=True) + w_own)
            w_all = jnp.concatenate(weights, axis=0)
            pltpu.make_async_copy(v_hbm.at[layer, rng], vbuf.at[rng], v_sem.at[i]).wait()
            picked = lax.dot_general(vbuf[rng].reshape(TILE_ROWS * head_dim, seq), w_all, (((1,), (1,)), ((), ())),
                                     preferred_element_type=F32)
            numer = jnp.zeros((head_dim, 4 * TILE_ROWS), F32)
            for b in range(TILE_ROWS):
                numer = jnp.where(col_row == b, picked[b * head_dim:(b + 1) * head_dim], numer)
            numer = numer.T
            values = vz[rng, :][:, :head_dim]
            heads = [((numer[g * TILE_ROWS:(g + 1) * TILE_ROWS] + selfs[g] * values) / sums[g]).astype(BF16)
                     for g in range(4)]
            attn[rng, :] = jnp.concatenate(heads, axis=1)

        part_tiles = size // TILE_ROWS

        def pair_of_tiles(i, carry):
            tile(p * part_tiles + 2 * i)
            tile(p * part_tiles + 2 * i + 1)
            return carry

        lax.fori_loop(0, part_tiles // 2, pair_of_tiles, 0)

    opened = [[] for _ in range(parts)]

    def start(p, copy):
        copy.start()
        opened[p].append(copy)

    def drain(p):
        for copy in opened[p]:
            copy.wait_send()
        opened[p] = []

    def arrived(ref, sem):
        remote(ref, ref, rs_send.at[0, 0], sem, me).wait_recv()

    def scatter(p, lhs, weight):
        drain(p)
        for index, target in enumerate((far, right, left, chip)):
            cols = pl.ds(pl.multiple_of(target * 2 * width, 128), 2 * width)
            block = dot(lhs, weight[:, cols]).astype(BF16)
            block_out[p, index, 0] = block[:, :width]
            block_out[p, index, 1] = block[:, width:]
            if index < 3:
                for k in range(2):
                    start(p, remote(block_out.at[p, index, k], block_in.at[p, me], rs_send.at[p, 2 * index + k],
                                    rs_recv.at[p, me], target * 2 + k))
            else:
                start(p, remote(block_out.at[p, index, other], block_in.at[p, me], rs_send.at[p, 6], rs_recv.at[p, me],
                                sibling))

    def add_up(p, own_rows):
        total = own_rows.astype(F32) + block_out[p, 3, core].astype(F32)
        for source in (sibling, right * 2 + core, left * 2 + core, right * 2 + other, left * 2 + other,
                       far * 2 + core, far * 2 + other):
            arrived(block_in.at[p, source], rs_recv.at[p, source])
            total = total + block_in[p, source].astype(F32)
        xg[me, ranges[p]] = total.astype(BF16)
        mine = xg.at[me, ranges[p]]
        for index, target in enumerate((far * 2 + core, right * 2 + core, left * 2 + core, sibling)):
            start(p, remote(mine, mine, ag_send.at[p, index], ag_recv.at[p, me], target))

    def forward(p):
        for index, source in enumerate((right * 2 + core, left * 2 + core, far * 2 + core)):
            piece = xg.at[source, ranges[p]]
            arrived(piece, ag_recv.at[p, source])
            start(p, remote(piece, piece, ag_send.at[p, 4 + index], ag_recv.at[p, source], sibling))

    def gathered(p):
        for source in (sibling, right * 2 + other, left * 2 + other, far * 2 + other):
            arrived(xg.at[source, ranges[p]], ag_recv.at[p, source])

    def residual(p, stage):
        if stage == 0:
            return lambda i: x_in[ranges[p], i * width:(i + 1) * width].astype(F32)
        return lambda i: xg[i, ranges[p]].astype(F32)

    def compute(p, stage, hook):
        layer, which = stage // 2, stage % 2
        gain = lambda cols: gains[which, layer:layer + 1, cols].astype(F32)
        if stage > 0:
            gathered(p)
        elif p == 0:
            ld_x.wait()
            for copy in ld_gain:
                copy.wait()
        rms_norm(p, residual(p, stage), gain)
        if which == 0:
            if p == 0:
                ld_q[layer].wait()
            attention(p, layer)
            hook()
            if p == 0:
                ld_o[layer].wait()
            scatter(p, attn[ranges[p], :], wo.at[layer])
            return
        if p == 0:
            ld_g[layer].wait()
            ld_u[layer].wait()
        n = normed[ranges[p], :]
        for c in range(0, act.shape[1], 256):
            if c * 2 == act.shape[1]:
                hook()
            g = dot(n, wg[layer, :, c:c + 256]).astype(BF16).astype(F32)
            u = dot(n, wu[layer, :, c:c + 256]).astype(BF16).astype(F32)
            act[ranges[p], c:c + 256] = (g * jax.nn.sigmoid(g) * u).astype(BF16)
        if p == 0:
            ld_d[layer].wait()
        scatter(p, act[ranges[p], :], wd.at[layer])

    own_cols = pl.ds(pl.multiple_of(me * width, 128), width)
    for stage in range(2 * layers):
        for p in range(parts):
            behind = stage > 0 and p + 1 < parts
            compute(p, stage, (lambda q=p + 1: forward(q)) if behind else (lambda: None))
        if stage == 0:
            for layer in range(layers):
                ld_g.append(load(w_gate.at[layer], wg.at[layer]))
                ld_u.append(load(w_up.at[layer], wu.at[layer]))
                ld_d.append(load(w_down.at[layer], wd.at[layer]))
                if layer + 1 < layers:
                    ld_q.append(load(w_qkv.at[layer + 1], wq.at[layer + 1]))
                    load_cache(layer + 1)
                    ld_o.append(load(w_out.at[layer + 1], wo.at[layer + 1]))
        for p in range(parts):
            add_up(p, x_in[ranges[p], own_cols] if stage == 0 else xg[me, ranges[p]])
        forward(0)
    for p in range(parts):
        if p > 0:
            forward(p)
        gathered(p)
        for i in range(group):
            out[ranges[p], i * width:(i + 1) * width] = xg[i, ranges[p]]
        drain(p)


PARTS = 2


def solution(mesh):
    group = mesh.shape["tp"]

    def local_step(hidden, lengths, k_cache, v_cache, attn_norm, w_qkv, w_out, mlp_norm, w_gate, w_up, w_down):
        rows, d_model = hidden.shape
        layers, _, seq, _, head_dim = k_cache.shape
        width = d_model // group
        size = rows // PARTS
        fused_width = w_qkv.shape[-1]
        n_tiles = rows // TILE_ROWS
        keys = jnp.transpose(k_cache, (0, 1, 3, 4, 2)).reshape(layers, rows, head_dim, seq)
        values = jnp.transpose(v_cache, (0, 1, 3, 4, 2)).reshape(layers, rows, head_dim, seq)
        w_qkv = w_qkv.reshape(layers, d_model, fused_width)
        any_spec = pl.BlockSpec(memory_space=pl.ANY)
        sem = pltpu.SemaphoreType.DMA
        n_loads = 4 + 5 * layers
        return pl.pallas_call(
            functools.partial(kernel, group, layers, PARTS),
            out_shape=jax.ShapeDtypeStruct((rows, d_model), BF16),
            in_specs=[any_spec] * 11,
            out_specs=pl.BlockSpec(memory_space=pltpu.VMEM),
            scratch_shapes=[
                pltpu.VMEM((rows, d_model), BF16),
                pltpu.VMEM((1, rows), jnp.int32),
                pltpu.VMEM((2, layers, d_model), BF16),
                pltpu.VMEM(w_qkv.shape, BF16),
                pltpu.VMEM(w_out.shape, BF16),
                pltpu.VMEM(w_gate.shape, BF16),
                pltpu.VMEM(w_up.shape, BF16),
                pltpu.VMEM(w_down.shape, BF16),
                pltpu.VMEM((rows, head_dim, seq), BF16),
                pltpu.VMEM((rows, head_dim, seq), BF16),
                pltpu.VMEM((rows, 128), F32),
                pltpu.VMEM((rows, 128), F32),
                pltpu.VMEM((rows, 128), F32),
                pltpu.VMEM((4, rows, 128), F32),
                pltpu.VMEM((rows, 128), F32),
                pltpu.VMEM((rows, 128), F32),
                pltpu.VMEM((rows, w_out.shape[1]), BF16),
                pltpu.VMEM((rows, d_model), BF16),
                pltpu.VMEM((rows, w_down.shape[1]), BF16),
                pltpu.VMEM((PARTS, 4, 2, size, width), BF16),
                pltpu.VMEM((PARTS, group, size, width), BF16),
                pltpu.VMEM((group, rows, width), BF16),
                sem((n_loads,)),
                sem((n_tiles,)),
                sem((n_tiles,)),
                sem((PARTS, 7)),
                sem((PARTS, group)),
                sem((PARTS, 7)),
                sem((PARTS, group)),
            ],
            compiler_params=pltpu.CompilerParams(
                collective_id=0, has_side_effects=True, vmem_limit_bytes=VMEM_MIB * 1024 * 1024),
            cost_estimate=pl.CostEstimate(flops=4 * 10**9, bytes_accessed=64 * 10**6, transcendentals=10**6),
            name="decode_layers",
        )(hidden, lengths.reshape(1, rows), keys, values, attn_norm, w_qkv, w_out, mlp_norm, w_gate, w_up, w_down)

    cache_spec = P(None, "dp", None, "tp", None)
    in_specs = (P("dp", None), P("dp"), cache_spec, cache_spec, P(), P(None, None, "tp", None),
                P(None, "tp", None), P(), P(None, None, "tp"), P(None, None, "tp"), P(None, "tp", None))
    return jax.shard_map(local_step, mesh=mesh, in_specs=in_specs, out_specs=P("dp", None), check_vma=False)
```

time: 98.2 us -> 82.8 us (0.84)
  Pallas kernels: 96.2 us -> 80.8 us
    pallas_call x1, Pallas kernels: 96.2 us -> 80.8 us  [local_step(): pl.pallas_call(functools.partial(kernel, group, layers, PARTS), out_shape...]
where the time goes in v2:
time: 82.8 us; the launch traced here: 82.7 us
  Pallas kernels  80.8 us (98%)
  local copies, waits for them, and re-layouts  1.88 us (2%)
    pallas_call x1, Pallas kernels, local_step(): pl.pallas_call(functools.partial(kernel, group, layers, PARTS), out_shape...  80.8 us
    unnamed x1, local copies, waits for them, and re-layouts  1.88 us

profile of v2, /device:TPU:81, one launch (start us, length us, event | category | flops | bytes accessed | tf_op | source)
XLA Modules:
  0.0 82.7 jit_solution(17184343171417918565)
XLA Ops:
  0.0 80.8 %decode_layers.1 = bf16[128,2048]{1,0:T(8,128)(2,1)} custom-call(bf16[128,2048]{1,0:T(8,128)(2,1)} %hidden.1, s32[1,128]{1,0:T(1,128)} %bitcast.15, bf16[2,128,64,512]{3,2,1,0:T(8,128)(2,1)} %bitcast.12, bf16[2,128,64,512]{3,2,1,0:T(8,128)(2,1)} %bitcast.13, bf16[2,2048]{1,0:T(2,128)(2,1)} %attn_norm.1, bf16[2,2048,384]{2,1,0:T(8,128)(2,1)} %bitcast.14, ...), custom_call_target="tpu_custom_call" | custom-call | flops 4000000000 | bytes 64000000 | tf_op jit(solution)/shard_map/decode_layers/pallas_call | solution.py:297
  80.8 1.9 %copy.15 = bf16[128,2048]{1,0:T(8,128)(2,1)} copy(bf16[128,2048]{1,0:T(8,128)(2,1)} %decode_layers.1) | data formatting | bytes 1048576

commit v3 on v2

--- a/solution.py
+++ b/solution.py
@@ -27,7 +27,7 @@
         device_id={"tp": device}, device_id_type=pl.DeviceIdType.MESH)
 
 
-def kernel(group, layers, parts,
+def kernel(group, layers, parts, stages,
            hidden, lengths, k_hbm, v_hbm, attn_norm, w_qkv, w_out, mlp_norm, w_gate, w_up, w_down, out,
            x_in, len_in, gains, wq, wo, wg, wu, wd, kbuf, vbuf,
            cos_tab, sin_tab, len_tab, qq, kz, vz, attn, normed, act,
@@ -55,24 +55,29 @@
         loads.append(copy)
         return copy
 
-    def load_cache(layer):
-        for i in range(n_tiles):
-            rng = pl.ds(i * TILE_ROWS, TILE_ROWS)
-            pltpu.make_async_copy(k_hbm.at[layer, rng], kbuf.at[rng], k_sem.at[i]).start()
-            pltpu.make_async_copy(v_hbm.at[layer, rng], vbuf.at[rng], v_sem.at[i]).start()
+    part_tiles = size // TILE_ROWS
+
+    def cache_copies(layer, i):
+        rng = pl.ds(i * TILE_ROWS, TILE_ROWS)
+        return (pltpu.make_async_copy(k_hbm.at[layer, rng], kbuf.at[rng], k_sem.at[i]),
+                pltpu.make_async_copy(v_hbm.at[layer, rng], vbuf.at[rng], v_sem.at[i]))
+
+    def load_cache(layer, tiles):
+        for i in tiles:
+            for copy in cache_copies(layer, i):
+                copy.start()
 
     ld_len = load(lengths, len_in)
     ld_x = load(hidden, x_in)
     ld_gain = [load(attn_norm, gains.at[0]), load(mlp_norm, gains.at[1])]
     ld_q = [load(w_qkv.at[0], wq.at[0])]
-    load_cache(0)
+    load_cache(0, range(part_tiles))
     ld_o = [load(w_out.at[0], wo.at[0])]
     ld_g, ld_u, ld_d = [], [], []
 
     barrier = pltpu.get_barrier_semaphore()
     for step in range(1, group):
         pl.semaphore_signal(barrier, inc=1, device_id={"tp": (me + step) % group}, device_id_type=pl.DeviceIdType.MESH)
-    pl.semaphore_wait(barrier, group - 1)
 
     ld_len.wait()
     len_row = jnp.broadcast_to(len_in[...].astype(F32), (rows, rows))
@@ -93,7 +98,7 @@
             cols = slice(i * width, (i + 1) * width)
             normed[ranges[p], cols] = (pieces(i) * scale * gain_row(cols)).astype(BF16)
 
-    def attention(p, layer):
+    def attention(p, layer, hook):
         part = ranges[p]
         fused = dot(normed[part, :], wq[layer]).astype(BF16).astype(F32)
         lane = lax.broadcasted_iota(jnp.int32, (size, 128), 1)
@@ -120,12 +125,13 @@
         col_row = lax.broadcasted_iota(jnp.int32, (head_dim, 4 * TILE_ROWS), 1) % TILE_ROWS
 
         def tile(i):
-            rng = pl.ds(pl.multiple_of(i * TILE_ROWS, TILE_ROWS), TILE_ROWS)
+            rng = pl.ds(i * TILE_ROWS, TILE_ROWS)
+            keys_in, values_in = cache_copies(layer, i)
             queries = [qq[g, rng, :] for g in range(4)]
             lhs = jnp.concatenate([
                 jnp.concatenate([jnp.where(row16 == 2 * j + high16, q, 0.0).astype(BF16) for j in range(TILE_ROWS // 2)], axis=1)
                 for q in queries], axis=0)
-            pltpu.make_async_copy(k_hbm.at[layer, rng], kbuf.at[rng], k_sem.at[i]).wait()
+            keys_in.wait()
             logits = dot(lhs, kbuf[rng].reshape(TILE_ROWS * head_dim, seq)) * head_dim ** -0.5
             live = pos < jnp.concatenate([len_tab[rng, :]] * (seq // 128), axis=1)
             keys = kz[rng, :]
@@ -140,7 +146,9 @@
                 selfs.append(w_own)
                 sums.append(jnp.sum(w.astype(F32), axis=1, keepdims=True) + w_own)
             w_all = jnp.concatenate(weights, axis=0)
-            pltpu.make_async_copy(v_hbm.at[layer, rng], vbuf.at[rng], v_sem.at[i]).wait()
+            values_in.wait()
+            if layer == 0 and i + part_tiles < n_tiles:
+                load_cache(0, [i + part_tiles])
             picked = lax.dot_general(vbuf[rng].reshape(TILE_ROWS * head_dim, seq), w_all, (((1,), (1,)), ((), ())),
                                      preferred_element_type=F32)
             numer = jnp.zeros((head_dim, 4 * TILE_ROWS), F32)
@@ -152,16 +160,13 @@
                      for g in range(4)]
             attn[rng, :] = jnp.concatenate(heads, axis=1)
 
-        part_tiles = size // TILE_ROWS
-
-        def pair_of_tiles(i, carry):
-            tile(p * part_tiles + 2 * i)
-            tile(p * part_tiles + 2 * i + 1)
-            return carry
-
-        lax.fori_loop(0, part_tiles // 2, pair_of_tiles, 0)
+        for t in range(part_tiles):
+            if 2 * t == part_tiles:
+                hook()
+            tile(p * part_tiles + t)
 
     opened = [[] for _ in range(parts)]
+    entered = []
 
     def start(p, copy):
         copy.start()
@@ -177,6 +182,9 @@
 
     def scatter(p, lhs, weight):
         drain(p)
+        if not entered:
+            pl.semaphore_wait(barrier, group - 1)
+            entered.append(True)
         for index, target in enumerate((far, right, left, chip)):
             cols = pl.ds(pl.multiple_of(target * 2 * width, 128), 2 * width)
             block = dot(lhs, weight[:, cols]).astype(BF16)
@@ -229,8 +237,7 @@
         if which == 0:
             if p == 0:
                 ld_q[layer].wait()
-            attention(p, layer)
-            hook()
+            attention(p, layer, hook)
             if p == 0:
                 ld_o[layer].wait()
             scatter(p, attn[ranges[p], :], wo.at[layer])
@@ -250,29 +257,43 @@
         scatter(p, act[ranges[p], :], wd.at[layer])
 
     own_cols = pl.ds(pl.multiple_of(me * width, 128), width)
-    for stage in range(2 * layers):
-        for p in range(parts):
-            behind = stage > 0 and p + 1 < parts
-            compute(p, stage, (lambda q=p + 1: forward(q)) if behind else (lambda: None))
+
+    def finish(p, stage):
+        add_up(p, x_in[ranges[p], own_cols] if stage == 0 else xg[me, ranges[p]])
+
+    def load_weights(layer):
+        ld_g.append(load(w_gate.at[layer], wg.at[layer]))
+        ld_u.append(load(w_up.at[layer], wu.at[layer]))
+        ld_d.append(load(w_down.at[layer], wd.at[layer]))
+
+    ahead, behind = 0, 1
+    for stage in range(stages):
+        layer, following = stage // 2, stage + 1 < stages
+        compute(ahead, stage, (lambda: finish(behind, stage - 1)) if stage > 0 else (lambda: None))
+        if stage % 2 == 1 and following:
+            ld_q.append(load(w_qkv.at[layer + 1], wq.at[layer + 1]))
+            load_cache(layer + 1, range(n_tiles))
+            ld_o.append(load(w_out.at[layer + 1], wo.at[layer + 1]))
+        if stage > 0:
+            forward(behind)
+        if stage % 2 == 0 and stage > 0:
+            load_weights(layer)
+        compute(behind, stage, (lambda: finish(ahead, stage)) if stage > 0 else (lambda: None))
         if stage == 0:
-            for layer in range(layers):
-                ld_g.append(load(w_gate.at[layer], wg.at[layer]))
-                ld_u.append(load(w_up.at[layer], wu.at[layer]))
-                ld_d.append(load(w_down.at[layer], wd.at[layer]))
-                if layer + 1 < layers:
-                    ld_q.append(load(w_qkv.at[layer + 1], wq.at[layer + 1]))
-                    load_cache(layer + 1)
-                    ld_o.append(load(w_out.at[layer + 1], wo.at[layer + 1]))
-        for p in range(parts):
-            add_up(p, x_in[ranges[p], own_cols] if stage == 0 else xg[me, ranges[p]])
-        forward(0)
-    for p in range(parts):
-        if p > 0:
-            forward(p)
+            load_weights(layer)
+            finish(ahead, stage)
+        forward(ahead)
+    finish(behind, stages - 1)
+
+    def emit(p):
         gathered(p)
         for i in range(group):
             out[ranges[p], i * width:(i + 1) * width] = xg[i, ranges[p]]
         drain(p)
+
+    emit(ahead)
+    forward(behind)
+    emit(behind)
 
 
 PARTS = 2
@@ -295,8 +316,8 @@
         sem = pltpu.SemaphoreType.DMA
         n_loads = 4 + 5 * layers
         return pl.pallas_call(
-            functools.partial(kernel, group, layers, PARTS),
-            out_shape=jax.ShapeDtypeStruct((rows, d_model), BF16),
+            functools.partial(kernel, group, layers, PARTS, 2 * layers),
+            out_shape=pltpu.VMEM((rows, d_model), BF16),
             in_specs=[any_spec] * 11,
             out_specs=pl.BlockSpec(memory_space=pltpu.VMEM),
             scratch_shapes=[

time: 82.8 us -> 79.6 us (0.961)
  Pallas kernels: 80.8 us -> 78.7 us
  local copies, waits for them, and re-layouts: 1.88 us -> 0.8 us
    pallas_call x1, Pallas kernels: 80.8 us -> 78.7 us  [local_step(): pl.pallas_call(functools.partial(kernel, group, layers, PARTS, 2 * layers...]
    unnamed x1, local copies, waits for them, and re-layouts: 1.88 us -> 0.8 us
where the time goes in v3:
time: 79.6 us; the launch traced here: 79.5 us
  Pallas kernels  78.7 us (99%)
  local copies, waits for them, and re-layouts  0.8 us (1%)
    pallas_call x1, Pallas kernels, local_step(): pl.pallas_call(functools.partial(kernel, group, layers, PARTS, 2 * layers...  78.7 us

profile of v3, /device:TPU:81, one launch (start us, length us, event | category | flops | bytes accessed | tf_op | source)
XLA Modules:
  0.0 79.5 jit_solution(3602395663421635289)
XLA Ops:
  0.0 78.7 %decode_layers.1 = bf16[128,2048]{1,0:T(8,128)(2,1)S(1)} custom-call(bf16[128,2048]{1,0:T(8,128)(2,1)} %hidden.1, s32[1,128]{1,0:T(1,128)} %bitcast.15, bf16[2,128,64,512]{3,2,1,0:T(8,128)(2,1)} %bitcast.12, bf16[2,128,64,512]{3,2,1,0:T(8,128)(2,1)} %bitcast.13, bf16[2,2048]{1,0:T(2,128)(2,1)} %attn_norm.1, bf16[2,2048,384]{2,1,0:T(8,128)(2,1)} %bitcast.14, ...), custom_call_target="tpu_custom_call" | custom-call | flops 4000000000 | bytes 64000000 | tf_op jit(solution)/shard_map/decode_layers/pallas_call | solution.py:318
  78.7 0.8 %copy.15 = bf16[128,2048]{1,0:T(8,128)(2,1)} copy(bf16[128,2048]{1,0:T(8,128)(2,1)S(1)} %decode_layers.1) | data formatting | bytes 1048576

commit v4 on v3

--- a/solution.py
+++ b/solution.py
@@ -21,6 +21,160 @@
     return jnp.dot(a, b, preferred_element_type=F32)
 
 
+def write_tables(len_in, len_tab, cos_tab, sin_tab, head_dim):
+    rows = len_in.shape[1]
+    len_row = jnp.broadcast_to(len_in[...].astype(F32), (rows, rows))
+    len_tab[...] = len_row.T
+    freq = lax.broadcasted_iota(jnp.int32, (head_dim // 2, rows), 0).astype(F32)
+    angles = len_row[:head_dim // 2] * jnp.exp(freq * (-2.0 / head_dim * math.log(ROPE_BASE)))
+    cosine, sine = jnp.cos(angles), jnp.sin(angles)
+    cos_tab[...] = jnp.concatenate([cosine] * 4, axis=0).T
+    sin_tab[...] = jnp.concatenate([-sine, sine, -sine, sine], axis=0).T
+
+
+def write_normed(normed, part, group, pieces, gain_row):
+    width = normed.shape[1] // group
+    total = jnp.zeros((part.size, 1), F32)
+    for i in range(group):
+        wide = pieces(i)
+        total = total + jnp.sum(wide * wide, axis=1, keepdims=True)
+    scale = lax.rsqrt(total / normed.shape[1] + NORM_EPS)
+    for i in range(group):
+        cols = slice(i * width, (i + 1) * width)
+        normed[part, cols] = (pieces(i) * scale * gain_row(cols)).astype(BF16)
+
+
+def write_heads(fused, part, head_dim, cos_tab, sin_tab, qq, kz, vz):
+    lane = lax.broadcasted_iota(jnp.int32, (part.size, 128), 1)
+    first = lane % head_dim < head_dim // 2
+    low = lane < head_dim
+    cos, sin = cos_tab[part, :], sin_tab[part, :]
+
+    def rope(x):
+        swapped = jnp.where(first, pltpu.roll(x, 128 - head_dim // 2, 1), pltpu.roll(x, head_dim // 2, 1))
+        return (x * cos + swapped * sin).astype(BF16).astype(F32)
+
+    for pair in range(2):
+        x = rope(fused[:, pair * 128:(pair + 1) * 128])
+        swap = pltpu.roll(x, head_dim, 1)
+        qq[2 * pair, part] = jnp.where(low, x, swap)
+        qq[2 * pair + 1, part] = jnp.where(low, swap, x)
+    kv = fused[:, 256:384]
+    kz[part, :] = jnp.where(low, rope(kv), 0.0)
+    vz[part, :] = pltpu.roll(kv, head_dim, 1)
+
+
+def attend(rng, span, kbuf, vbuf, len_tab, qq, kz, vz, attn, keys_ready, values_ready):
+    head_dim = kbuf.shape[1]
+    row16 = lax.broadcasted_iota(jnp.int32, (TILE_ROWS, 128), 0)
+    high16 = lax.broadcasted_iota(jnp.int32, (TILE_ROWS, 128), 1) // head_dim
+    pos = lax.broadcasted_iota(jnp.int32, (TILE_ROWS, span), 1).astype(F32)
+    col_row = lax.broadcasted_iota(jnp.int32, (head_dim, 4 * TILE_ROWS), 1) % TILE_ROWS
+    queries = [qq[g, rng, :] for g in range(4)]
+    lhs = jnp.concatenate([
+        jnp.concatenate([jnp.where(row16 == 2 * j + high16, q, 0.0).astype(BF16) for j in range(TILE_ROWS // 2)], axis=1)
+        for q in queries], axis=0)
+    keys_ready()
+    logits = dot(lhs, kbuf[rng, :, :span].reshape(TILE_ROWS * head_dim, span)) * head_dim ** -0.5
+    live = pos < jnp.concatenate([len_tab[rng, :]] * (span // 128), axis=1)
+    keys = kz[rng, :]
+    weights, sums, selfs = [], [], []
+    for g in range(4):
+        s = jnp.where(live, logits[g * TILE_ROWS:(g + 1) * TILE_ROWS], NEG)
+        own = jnp.sum(queries[g] * keys, axis=1, keepdims=True) * head_dim ** -0.5
+        peak = jnp.maximum(jnp.max(s, axis=1, keepdims=True), own)
+        w = jnp.exp(s - peak).astype(BF16)
+        w_own = jnp.exp(own - peak).astype(BF16).astype(F32)
+        weights.append(w)
+        selfs.append(w_own)
+        sums.append(jnp.sum(w.astype(F32), axis=1, keepdims=True) + w_own)
+    w_all = jnp.concatenate(weights, axis=0)
+    values_ready()
+    picked = lax.dot_general(vbuf[rng, :, :span].reshape(TILE_ROWS * head_dim, span), w_all, (((1,), (1,)), ((), ())),
+                             preferred_element_type=F32)
+    numer = jnp.zeros((head_dim, 4 * TILE_ROWS), F32)
+    for b in range(TILE_ROWS):
+        numer = jnp.where(col_row == b, picked[b * head_dim:(b + 1) * head_dim], numer)
+    numer = numer.T
+    values = vz[rng, :][:, :head_dim]
+    heads = [((numer[g * TILE_ROWS:(g + 1) * TILE_ROWS] + selfs[g] * values) / sums[g]).astype(BF16) for g in range(4)]
+    attn[rng, :] = jnp.concatenate(heads, axis=1)
+
+
+def first_kernel(group, hidden, lengths, len_flat, k_hbm, v_hbm, attn_norm, w_qkv, attn,
+                 x_in, len_in, len_s, gains, wq, kbuf, vbuf, cos_tab, sin_tab, len_tab, qq, kz, vz, normed,
+                 load_sem, k_sem, v_sem):
+    rows, d_model = hidden.shape
+    width = d_model // group
+    head_dim, seq = kbuf.shape[1:]
+    n_tiles = rows // TILE_ROWS
+    everything = pl.ds(0, rows)
+    waits = []
+
+    def load(src, dst):
+        copy = pltpu.make_async_copy(src, dst, load_sem.at[len(waits)])
+        copy.start()
+        waits.append(copy)
+
+    def copies(rng, i, first):
+        cols = pl.ds(0, 128) if first else pl.ds(128, seq - 128)
+        slot = 0 if first else 1
+        return (pltpu.make_async_copy(k_hbm.at[0, rng, :, cols], kbuf.at[rng, :, cols], k_sem.at[slot, i]),
+                pltpu.make_async_copy(v_hbm.at[0, rng, :, cols], vbuf.at[rng, :, cols], v_sem.at[slot, i]))
+
+    load(len_flat, len_s)
+    load(lengths, len_in)
+    load(hidden, x_in)
+    load(attn_norm, gains)
+    load(w_qkv.at[0], wq)
+    for i in range(n_tiles):
+        for copy in copies(pl.ds(i * TILE_ROWS, TILE_ROWS), i, True):
+            copy.start()
+
+    def tile_is_long(i):
+        longest = len_s[i * TILE_ROWS]
+        for b in range(1, TILE_ROWS):
+            longest = jnp.maximum(longest, len_s[i * TILE_ROWS + b])
+        return longest > 128
+
+    waits[0].wait()
+    for i in range(n_tiles):
+        @pl.when(tile_is_long(i))
+        def _():
+            for copy in copies(pl.ds(i * TILE_ROWS, TILE_ROWS), i, False):
+                copy.start()
+    waits[1].wait()
+    write_tables(len_in, len_tab, cos_tab, sin_tab, head_dim)
+    waits[2].wait()
+    waits[3].wait()
+    write_normed(normed, everything, group, lambda i: x_in[:, i * width:(i + 1) * width].astype(F32),
+                 lambda cols: gains[0:1, cols].astype(F32))
+    waits[4].wait()
+    fused = dot(normed[...], wq[...]).astype(BF16).astype(F32)
+    write_heads(fused, everything, head_dim, cos_tab, sin_tab, qq, kz, vz)
+
+    def tile(i, carry):
+        rng = pl.ds(pl.multiple_of(i * TILE_ROWS, TILE_ROWS), TILE_ROWS)
+        long = tile_is_long(i)
+        keys_in, values_in = copies(rng, i, True)
+        keys_in.wait()
+        values_in.wait()
+
+        @pl.when(long)
+        def _():
+            for copy in copies(rng, i, False):
+                copy.wait()
+            attend(rng, seq, kbuf, vbuf, len_tab, qq, kz, vz, attn, lambda: None, lambda: None)
+
+        @pl.when(jnp.logical_not(long))
+        def _():
+            attend(rng, 128, kbuf, vbuf, len_tab, qq, kz, vz, attn, lambda: None, lambda: None)
+
+        return carry
+
+    lax.fori_loop(0, n_tiles, tile, 0)
+
+
 def remote(src, dst, send_sem, recv_sem, device):
     return pltpu.make_async_remote_copy(
         src_ref=src, dst_ref=dst, send_sem=send_sem, recv_sem=recv_sem,
@@ -28,7 +182,7 @@
 
 
 def kernel(group, layers, parts, stages,
-           hidden, lengths, k_hbm, v_hbm, attn_norm, w_qkv, w_out, mlp_norm, w_gate, w_up, w_down, out,
+           attn_first, hidden, lengths, k_hbm, v_hbm, attn_norm, w_qkv, w_out, mlp_norm, w_gate, w_up, w_down, out,
            x_in, len_in, gains, wq, wo, wg, wu, wd, kbuf, vbuf,
            cos_tab, sin_tab, len_tab, qq, kz, vz, attn, normed, act,
            block_out, block_in, xg,
@@ -67,103 +221,26 @@
             for copy in cache_copies(layer, i):
                 copy.start()
 
+    ld_q, ld_o = [None], [load(w_out.at[0], wo.at[0])]
     ld_len = load(lengths, len_in)
     ld_x = load(hidden, x_in)
     ld_gain = [load(attn_norm, gains.at[0]), load(mlp_norm, gains.at[1])]
-    ld_q = [load(w_qkv.at[0], wq.at[0])]
-    load_cache(0, range(part_tiles))
-    ld_o = [load(w_out.at[0], wo.at[0])]
     ld_g, ld_u, ld_d = [], [], []
 
     barrier = pltpu.get_barrier_semaphore()
     for step in range(1, group):
         pl.semaphore_signal(barrier, inc=1, device_id={"tp": (me + step) % group}, device_id_type=pl.DeviceIdType.MESH)
 
-    ld_len.wait()
-    len_row = jnp.broadcast_to(len_in[...].astype(F32), (rows, rows))
-    len_tab[...] = len_row.T
-    freq = lax.broadcasted_iota(jnp.int32, (head_dim // 2, rows), 0).astype(F32)
-    angles = len_row[:head_dim // 2] * jnp.exp(freq * (-2.0 / head_dim * math.log(ROPE_BASE)))
-    cosine, sine = jnp.cos(angles), jnp.sin(angles)
-    cos_tab[...] = jnp.concatenate([cosine] * 4, axis=0).T
-    sin_tab[...] = jnp.concatenate([-sine, sine, -sine, sine], axis=0).T
-
-    def rms_norm(p, pieces, gain_row):
-        total = jnp.zeros((size, 1), F32)
-        for i in range(group):
-            wide = pieces(i)
-            total = total + jnp.sum(wide * wide, axis=1, keepdims=True)
-        scale = lax.rsqrt(total / d_model + NORM_EPS)
-        for i in range(group):
-            cols = slice(i * width, (i + 1) * width)
-            normed[ranges[p], cols] = (pieces(i) * scale * gain_row(cols)).astype(BF16)
-
     def attention(p, layer, hook):
         part = ranges[p]
         fused = dot(normed[part, :], wq[layer]).astype(BF16).astype(F32)
-        lane = lax.broadcasted_iota(jnp.int32, (size, 128), 1)
-        first = lane % head_dim < head_dim // 2
-        low = lane < head_dim
-        cos, sin = cos_tab[part, :], sin_tab[part, :]
-
-        def rope(x):
-            swapped = jnp.where(first, pltpu.roll(x, 128 - head_dim // 2, 1), pltpu.roll(x, head_dim // 2, 1))
-            return (x * cos + swapped * sin).astype(BF16).astype(F32)
-
-        for pair in range(2):
-            x = rope(fused[:, pair * 128:(pair + 1) * 128])
-            swap = pltpu.roll(x, head_dim, 1)
-            qq[2 * pair, part] = jnp.where(low, x, swap)
-            qq[2 * pair + 1, part] = jnp.where(low, swap, x)
-        kv = fused[:, 256:384]
-        kz[part, :] = jnp.where(low, rope(kv), 0.0)
-        vz[part, :] = pltpu.roll(kv, head_dim, 1)
-
-        row16 = lax.broadcasted_iota(jnp.int32, (TILE_ROWS, 128), 0)
-        high16 = lax.broadcasted_iota(jnp.int32, (TILE_ROWS, 128), 1) // head_dim
-        pos = lax.broadcasted_iota(jnp.int32, (TILE_ROWS, seq), 1).astype(F32)
-        col_row = lax.broadcasted_iota(jnp.int32, (head_dim, 4 * TILE_ROWS), 1) % TILE_ROWS
-
-        def tile(i):
-            rng = pl.ds(i * TILE_ROWS, TILE_ROWS)
-            keys_in, values_in = cache_copies(layer, i)
-            queries = [qq[g, rng, :] for g in range(4)]
-            lhs = jnp.concatenate([
-                jnp.concatenate([jnp.where(row16 == 2 * j + high16, q, 0.0).astype(BF16) for j in range(TILE_ROWS // 2)], axis=1)
-                for q in queries], axis=0)
-            keys_in.wait()
-            logits = dot(lhs, kbuf[rng].reshape(TILE_ROWS * head_dim, seq)) * head_dim ** -0.5
-            live = pos < jnp.concatenate([len_tab[rng, :]] * (seq // 128), axis=1)
-            keys = kz[rng, :]
-            weights, sums, selfs = [], [], []
-            for g in range(4):
-                s = jnp.where(live, logits[g * TILE_ROWS:(g + 1) * TILE_ROWS], NEG)
-                own = jnp.sum(queries[g] * keys, axis=1, keepdims=True) * head_dim ** -0.5
-                peak = jnp.maximum(jnp.max(s, axis=1, keepdims=True), own)
-                w = jnp.exp(s - peak).astype(BF16)
-                w_own = jnp.exp(own - peak).astype(BF16).astype(F32)
-                weights.append(w)
-                selfs.append(w_own)
-                sums.append(jnp.sum(w.astype(F32), axis=1, keepdims=True) + w_own)
-            w_all = jnp.concatenate(weights, axis=0)
-            values_in.wait()
-            if layer == 0 and i + part_tiles < n_tiles:
-                load_cache(0, [i + part_tiles])
-            picked = lax.dot_general(vbuf[rng].reshape(TILE_ROWS * head_dim, seq), w_all, (((1,), (1,)), ((), ())),
-                                     preferred_element_type=F32)
-            numer = jnp.zeros((head_dim, 4 * TILE_ROWS), F32)
-            for b in range(TILE_ROWS):
-                numer = jnp.where(col_row == b, picked[b * head_dim:(b + 1) * head_dim], numer)
-            numer = numer.T
-            values = vz[rng, :][:, :head_dim]
-            heads = [((numer[g * TILE_ROWS:(g + 1) * TILE_ROWS] + selfs[g] * values) / sums[g]).astype(BF16)
-                     for g in range(4)]
-            attn[rng, :] = jnp.concatenate(heads, axis=1)
-
+        write_heads(fused, part, head_dim, cos_tab, sin_tab, qq, kz, vz)
         for t in range(part_tiles):
             if 2 * t == part_tiles:
                 hook()
-            tile(p * part_tiles + t)
+            i = p * part_tiles + t
+            keys_in, values_in = cache_copies(layer, i)
+            attend(pl.ds(i * TILE_ROWS, TILE_ROWS), seq, kbuf, vbuf, len_tab, qq, kz, vz, attn, keys_in.wait, values_in.wait)
 
     opened = [[] for _ in range(parts)]
     entered = []
@@ -219,21 +296,16 @@
         for source in (sibling, right * 2 + other, left * 2 + other, far * 2 + other):
             arrived(xg.at[source, ranges[p]], ag_recv.at[p, source])
 
-    def residual(p, stage):
-        if stage == 0:
-            return lambda i: x_in[ranges[p], i * width:(i + 1) * width].astype(F32)
-        return lambda i: xg[i, ranges[p]].astype(F32)
-
     def compute(p, stage, hook):
         layer, which = stage // 2, stage % 2
         gain = lambda cols: gains[which, layer:layer + 1, cols].astype(F32)
-        if stage > 0:
-            gathered(p)
-        elif p == 0:
-            ld_x.wait()
-            for copy in ld_gain:
-                copy.wait()
-        rms_norm(p, residual(p, stage), gain)
+        if stage == 0:
+            if p == 0:
+                ld_o[0].wait()
+            scatter(p, attn_first[ranges[p], :], wo.at[0])
+            return
+        gathered(p)
+        write_normed(normed, ranges[p], group, lambda i: xg[i, ranges[p]].astype(F32), gain)
         if which == 0:
             if p == 0:
                 ld_q[layer].wait()
@@ -281,6 +353,10 @@
         compute(behind, stage, (lambda: finish(ahead, stage)) if stage > 0 else (lambda: None))
         if stage == 0:
             load_weights(layer)
+            ld_len.wait()
+            write_tables(len_in, len_tab, cos_tab, sin_tab, head_dim)
+            for copy in [ld_x] + ld_gain:
+                copy.wait()
             finish(ahead, stage)
         forward(ahead)
     finish(behind, stages - 1)
@@ -314,11 +390,41 @@
         w_qkv = w_qkv.reshape(layers, d_model, fused_width)
         any_spec = pl.BlockSpec(memory_space=pl.ANY)
         sem = pltpu.SemaphoreType.DMA
+        vmem = pltpu.VMEM
+        attn_first = pl.pallas_call(
+            functools.partial(first_kernel, group),
+            out_shape=pltpu.VMEM((rows, w_out.shape[1]), BF16),
+            in_specs=[any_spec] * 7,
+            out_specs=pl.BlockSpec(memory_space=pltpu.VMEM),
+            scratch_shapes=[
+                vmem((rows, d_model), BF16),
+                vmem((1, rows), jnp.int32),
+                pltpu.SMEM((rows,), jnp.int32),
+                vmem((layers, d_model), BF16),
+                vmem((d_model, fused_width), BF16),
+                vmem((rows, head_dim, seq), BF16),
+                vmem((rows, head_dim, seq), BF16),
+                vmem((rows, 128), F32),
+                vmem((rows, 128), F32),
+                vmem((rows, 128), F32),
+                vmem((4, rows, 128), F32),
+                vmem((rows, 128), F32),
+                vmem((rows, 128), F32),
+                vmem((rows, d_model), BF16),
+                sem((5,)),
+                sem((2, n_tiles)),
+                sem((2, n_tiles)),
+            ],
+            compiler_params=pltpu.CompilerParams(vmem_limit_bytes=63 * 1024 * 1024),
+            cost_estimate=pl.CostEstimate(flops=10**9, bytes_accessed=10**7, transcendentals=10**6),
+            name="first_attention",
+        )(hidden, lengths.reshape(1, rows), lengths, keys, values, attn_norm, w_qkv)
+        attn_first = pltpu.with_memory_space_constraint(attn_first, pltpu.VMEM)
         n_loads = 4 + 5 * layers
         return pl.pallas_call(
             functools.partial(kernel, group, layers, PARTS, 2 * layers),
             out_shape=pltpu.VMEM((rows, d_model), BF16),
-            in_specs=[any_spec] * 11,
+            in_specs=[pl.BlockSpec(memory_space=pltpu.VMEM)] + [any_spec] * 11,
             out_specs=pl.BlockSpec(memory_space=pltpu.VMEM),
             scratch_shapes=[
                 pltpu.VMEM((rows, d_model), BF16),
@@ -355,7 +461,7 @@
                 collective_id=0, has_side_effects=True, vmem_limit_bytes=VMEM_MIB * 1024 * 1024),
             cost_estimate=pl.CostEstimate(flops=4 * 10**9, bytes_accessed=64 * 10**6, transcendentals=10**6),
             name="decode_layers",
-        )(hidden, lengths.reshape(1, rows), keys, values, attn_norm, w_qkv, w_out, mlp_norm, w_gate, w_up, w_down)
+        )(attn_first, hidden, lengths.reshape(1, rows), keys, values, attn_norm, w_qkv, w_out, mlp_norm, w_gate, w_up, w_down)
 
     cache_spec = P(None, "dp", None, "tp", None)
     in_specs = (P("dp", None), P("dp"), cache_spec, cache_spec, P(), P(None, None, "tp", None),

time: 79.6 us -> 78.5 us (0.986)
  Pallas kernels: 78.7 us -> 77.6 us
    pallas_call x1, Pallas kernels: 78.7 us -> 68.3 us  [local_step(): pl.pallas_call(functools.partial(kernel, group, layers, PARTS, 2 * layers...]
    pallas_call x0 -> x1, Pallas kernels: none -> 9.21 us  [local_step(): pl.pallas_call(functools.partial(first_kernel, group), out_shape=pltpu.VM...]
where the time goes in v4:
time: 78.5 us; the launch traced here: 78.4 us
  Pallas kernels  77.6 us (99%)
  local copies, waits for them, and re-layouts  0.8 us (1%)
    pallas_call x1, Pallas kernels, local_step(): pl.pallas_call(functools.partial(kernel, group, layers, PARTS, 2 * layers...  68.3 us
    pallas_call x1, Pallas kernels, local_step(): pl.pallas_call(functools.partial(first_kernel, group), out_shape=pltpu.VM...  9.21 us

profile of v4, /device:TPU:81, one launch (start us, length us, event | category | flops | bytes accessed | tf_op | source)
XLA Modules:
  0.0 78.4 jit_solution(9869582089627356979)
XLA Ops:
  0.0 9.2 %first_attention.1.attn_first = bf16[128,256]{1,0:T(8,128)(2,1)S(1)} custom-call(bf16[128,2048]{1,0:T(8,128)(2,1)} %hidden.3, s32[1,128]{1,0:T(1,128)} %bitcast.18, s32[128]{0:T(128)} %len_flat.1, bf16[2,128,64,512]{3,2,1,0:T(8,128)(2,1)} %bitcast.12, bf16[2,128,64,512]{3,2,1,0:T(8,128)(2,1)} %bitcast.14, bf16[2,2048]{1,0:T(2,128)(2,1)} %attn_norm.3, ...), custom_call_target="tpu_custom_call" | custom-call | flops 1000000000 | bytes 10000000 | tf_op jit(solution)/shard_map/first_attention/pallas_call | solution.py:394
  9.2 68.3 %decode_layers.1 = bf16[128,2048]{1,0:T(8,128)(2,1)S(1)} custom-call(bf16[128,256]{1,0:T(8,128)(2,1)S(1)} %first_attention.1.attn_first, bf16[128,2048]{1,0:T(8,128)(2,1)} %hidden.3, s32[1,128]{1,0:T(1,128)} %bitcast.19, bf16[2,128,64,512]{3,2,1,0:T(8,128)(2,1)} %bitcast.13, bf16[2,128,64,512]{3,2,1,0:T(8,128)(2,1)} %bitcast.15, bf16[2,2048]{1,0:T(2,128)(2,1)} %attn_norm.3, ...), custom_call_target="tpu_custom_call" | custom-call | flops 4000000000 | bytes 64000000 | tf_op jit(solution)/shard_map/decode_layers/pallas_call | solution.py:424
  77.6 0.8 %copy.15 = bf16[128,2048]{1,0:T(8,128)(2,1)} copy(bf16[128,2048]{1,0:T(8,128)(2,1)S(1)} %decode_layers.1) | data formatting | bytes 1048576

commit v5 on v4

--- a/solution.py
+++ b/solution.py
@@ -64,7 +64,7 @@
     vz[part, :] = pltpu.roll(kv, head_dim, 1)
 
 
-def attend(rng, span, kbuf, vbuf, len_tab, qq, kz, vz, attn, keys_ready, values_ready):
+def attend(rng, span, kbuf, vbuf, len_tab, qq, kz, vz, attn):
     head_dim = kbuf.shape[1]
     row16 = lax.broadcasted_iota(jnp.int32, (TILE_ROWS, 128), 0)
     high16 = lax.broadcasted_iota(jnp.int32, (TILE_ROWS, 128), 1) // head_dim
@@ -74,7 +74,6 @@
     lhs = jnp.concatenate([
         jnp.concatenate([jnp.where(row16 == 2 * j + high16, q, 0.0).astype(BF16) for j in range(TILE_ROWS // 2)], axis=1)
         for q in queries], axis=0)
-    keys_ready()
     logits = dot(lhs, kbuf[rng, :, :span].reshape(TILE_ROWS * head_dim, span)) * head_dim ** -0.5
     live = pos < jnp.concatenate([len_tab[rng, :]] * (span // 128), axis=1)
     keys = kz[rng, :]
@@ -89,7 +88,6 @@
         selfs.append(w_own)
         sums.append(jnp.sum(w.astype(F32), axis=1, keepdims=True) + w_own)
     w_all = jnp.concatenate(weights, axis=0)
-    values_ready()
     picked = lax.dot_general(vbuf[rng, :, :span].reshape(TILE_ROWS * head_dim, span), w_all, (((1,), (1,)), ((), ())),
                              preferred_element_type=F32)
     numer = jnp.zeros((head_dim, 4 * TILE_ROWS), F32)
@@ -101,8 +99,8 @@
     attn[rng, :] = jnp.concatenate(heads, axis=1)
 
 
-def first_kernel(group, hidden, lengths, len_flat, k_hbm, v_hbm, attn_norm, w_qkv, attn,
-                 x_in, len_in, len_s, gains, wq, kbuf, vbuf, cos_tab, sin_tab, len_tab, qq, kz, vz, normed,
+def first_kernel(group, hidden, lengths, len_flat, k_hbm, v_hbm, attn_norm, w_qkv, w_out, blocks,
+                 attn, x_in, len_in, len_s, gains, wq, wo, kbuf, vbuf, cos_tab, sin_tab, len_tab, qq, kz, vz, normed,
                  load_sem, k_sem, v_sem):
     rows, d_model = hidden.shape
     width = d_model // group
@@ -143,6 +141,7 @@
         def _():
             for copy in copies(pl.ds(i * TILE_ROWS, TILE_ROWS), i, False):
                 copy.start()
+    load(w_out.at[0], wo)
     waits[1].wait()
     write_tables(len_in, len_tab, cos_tab, sin_tab, head_dim)
     waits[2].wait()
@@ -153,26 +152,31 @@
     fused = dot(normed[...], wq[...]).astype(BF16).astype(F32)
     write_heads(fused, everything, head_dim, cos_tab, sin_tab, qq, kz, vz)
 
-    def tile(i, carry):
+    for i in range(n_tiles):
+        for copy in copies(pl.ds(i * TILE_ROWS, TILE_ROWS), i, True):
+            copy.wait()
+    for i in range(n_tiles):
+        attend(pl.ds(i * TILE_ROWS, TILE_ROWS), 128, kbuf, vbuf, len_tab, qq, kz, vz, attn)
+
+    def long_tile(i, carry):
         rng = pl.ds(pl.multiple_of(i * TILE_ROWS, TILE_ROWS), TILE_ROWS)
-        long = tile_is_long(i)
-        keys_in, values_in = copies(rng, i, True)
-        keys_in.wait()
-        values_in.wait()
-
-        @pl.when(long)
+
+        @pl.when(tile_is_long(i))
         def _():
             for copy in copies(rng, i, False):
                 copy.wait()
-            attend(rng, seq, kbuf, vbuf, len_tab, qq, kz, vz, attn, lambda: None, lambda: None)
-
-        @pl.when(jnp.logical_not(long))
-        def _():
-            attend(rng, 128, kbuf, vbuf, len_tab, qq, kz, vz, attn, lambda: None, lambda: None)
+            attend(rng, seq, kbuf, vbuf, len_tab, qq, kz, vz, attn)
 
         return carry
 
-    lax.fori_loop(0, n_tiles, tile, 0)
+    lax.fori_loop(0, n_tiles, long_tile, 0)
+    waits[5].wait()
+    parts, chips, _, size, _ = blocks.shape
+    for p in range(parts):
+        for target in range(chips):
+            block = dot(attn[p * size:(p + 1) * size, :], wo[:, target * 2 * width:(target + 1) * 2 * width]).astype(BF16)
+            blocks[p, target, 0] = block[:, :width]
+            blocks[p, target, 1] = block[:, width:]
 
 
 def remote(src, dst, send_sem, recv_sem, device):
@@ -182,7 +186,7 @@
 
 
 def kernel(group, layers, parts, stages,
-           attn_first, hidden, lengths, k_hbm, v_hbm, attn_norm, w_qkv, w_out, mlp_norm, w_gate, w_up, w_down, out,
+           blocks, hidden, lengths, k_hbm, v_hbm, attn_norm, w_qkv, w_out, mlp_norm, w_gate, w_up, w_down, out,
            x_in, len_in, gains, wq, wo, wg, wu, wd, kbuf, vbuf,
            cos_tab, sin_tab, len_tab, qq, kz, vz, attn, normed, act,
            block_out, block_in, xg,
@@ -221,7 +225,7 @@
             for copy in cache_copies(layer, i):
                 copy.start()
 
-    ld_q, ld_o = [None], [load(w_out.at[0], wo.at[0])]
+    ld_q, ld_o = [None], [None]
     ld_len = load(lengths, len_in)
     ld_x = load(hidden, x_in)
     ld_gain = [load(attn_norm, gains.at[0]), load(mlp_norm, gains.at[1])]
@@ -235,15 +239,16 @@
         part = ranges[p]
         fused = dot(normed[part, :], wq[layer]).astype(BF16).astype(F32)
         write_heads(fused, part, head_dim, cos_tab, sin_tab, qq, kz, vz)
-        for t in range(part_tiles):
-            if 2 * t == part_tiles:
+        tiles = range(p * part_tiles, (p + 1) * part_tiles)
+        for i in tiles:
+            for copy in cache_copies(layer, i):
+                copy.wait()
+        for i in tiles:
+            if 2 * (i - tiles[0]) == part_tiles:
                 hook()
-            i = p * part_tiles + t
-            keys_in, values_in = cache_copies(layer, i)
-            attend(pl.ds(i * TILE_ROWS, TILE_ROWS), seq, kbuf, vbuf, len_tab, qq, kz, vz, attn, keys_in.wait, values_in.wait)
+            attend(pl.ds(i * TILE_ROWS, TILE_ROWS), seq, kbuf, vbuf, len_tab, qq, kz, vz, attn)
 
     opened = [[] for _ in range(parts)]
-    entered = []
 
     def start(p, copy):
         copy.start()
@@ -257,26 +262,25 @@
     def arrived(ref, sem):
         remote(ref, ref, rs_send.at[0, 0], sem, me).wait_recv()
 
+    def send_blocks(p, index, target, pair):
+        if index < 3:
+            for k in range(2):
+                start(p, remote(pair.at[k], block_in.at[p, me], rs_send.at[p, 2 * index + k], rs_recv.at[p, me],
+                                target * 2 + k))
+        else:
+            start(p, remote(pair.at[other], block_in.at[p, me], rs_send.at[p, 6], rs_recv.at[p, me], sibling))
+
     def scatter(p, lhs, weight):
         drain(p)
-        if not entered:
-            pl.semaphore_wait(barrier, group - 1)
-            entered.append(True)
         for index, target in enumerate((far, right, left, chip)):
             cols = pl.ds(pl.multiple_of(target * 2 * width, 128), 2 * width)
             block = dot(lhs, weight[:, cols]).astype(BF16)
             block_out[p, index, 0] = block[:, :width]
             block_out[p, index, 1] = block[:, width:]
-            if index < 3:
-                for k in range(2):
-                    start(p, remote(block_out.at[p, index, k], block_in.at[p, me], rs_send.at[p, 2 * index + k],
-                                    rs_recv.at[p, me], target * 2 + k))
-            else:
-                start(p, remote(block_out.at[p, index, other], block_in.at[p, me], rs_send.at[p, 6], rs_recv.at[p, me],
-                                sibling))
-
-    def add_up(p, own_rows):
-        total = own_rows.astype(F32) + block_out[p, 3, core].astype(F32)
+            send_blocks(p, index, target, block_out.at[p, index])
+
+    def add_up(p, own_rows, own_block):
+        total = own_rows.astype(F32) + own_block.astype(F32)
         for source in (sibling, right * 2 + core, left * 2 + core, right * 2 + other, left * 2 + other,
                        far * 2 + core, far * 2 + other):
             arrived(block_in.at[p, source], rs_recv.at[p, source])
@@ -301,8 +305,9 @@
         gain = lambda cols: gains[which, layer:layer + 1, cols].astype(F32)
         if stage == 0:
             if p == 0:
-                ld_o[0].wait()
-            scatter(p, attn_first[ranges[p], :], wo.at[0])
+                pl.semaphore_wait(barrier, group - 1)
+            for index, target in enumerate((far, right, left, chip)):
+                send_blocks(p, index, target, blocks.at[p, target])
             return
         gathered(p)
         write_normed(normed, ranges[p], group, lambda i: xg[i, ranges[p]].astype(F32), gain)
@@ -331,7 +336,10 @@
     own_cols = pl.ds(pl.multiple_of(me * width, 128), width)
 
     def finish(p, stage):
-        add_up(p, x_in[ranges[p], own_cols] if stage == 0 else xg[me, ranges[p]])
+        if stage == 0:
+            add_up(p, x_in[ranges[p], own_cols], blocks[p, chip, core])
+        else:
+            add_up(p, xg[me, ranges[p]], block_out[p, 3, core])
 
     def load_weights(layer):
         ld_g.append(load(w_gate.at[layer], wg.at[layer]))
@@ -391,17 +399,19 @@
         any_spec = pl.BlockSpec(memory_space=pl.ANY)
         sem = pltpu.SemaphoreType.DMA
         vmem = pltpu.VMEM
-        attn_first = pl.pallas_call(
+        blocks = pl.pallas_call(
             functools.partial(first_kernel, group),
-            out_shape=pltpu.VMEM((rows, w_out.shape[1]), BF16),
-            in_specs=[any_spec] * 7,
+            out_shape=pltpu.VMEM((PARTS, group // 2, 2, size, width), BF16),
+            in_specs=[any_spec] * 8,
             out_specs=pl.BlockSpec(memory_space=pltpu.VMEM),
             scratch_shapes=[
+                vmem((rows, w_out.shape[1]), BF16),
                 vmem((rows, d_model), BF16),
                 vmem((1, rows), jnp.int32),
                 pltpu.SMEM((rows,), jnp.int32),
                 vmem((layers, d_model), BF16),
                 vmem((d_model, fused_width), BF16),
+                vmem(w_out.shape[1:], BF16),
                 vmem((rows, head_dim, seq), BF16),
                 vmem((rows, head_dim, seq), BF16),
                 vmem((rows, 128), F32),
@@ -411,16 +421,16 @@
                 vmem((rows, 128), F32),
                 vmem((rows, 128), F32),
                 vmem((rows, d_model), BF16),
-                sem((5,)),
+                sem((6,)),
                 sem((2, n_tiles)),
                 sem((2, n_tiles)),
             ],
             compiler_params=pltpu.CompilerParams(vmem_limit_bytes=63 * 1024 * 1024),
             cost_estimate=pl.CostEstimate(flops=10**9, bytes_accessed=10**7, transcendentals=10**6),
             name="first_attention",
-        )(hidden, lengths.reshape(1, rows), lengths, keys, values, attn_norm, w_qkv)
-        attn_first = pltpu.with_memory_space_constraint(attn_first, pltpu.VMEM)
-        n_loads = 4 + 5 * layers
+        )(hidden, lengths.reshape(1, rows), lengths, keys, values, attn_norm, w_qkv, w_out)
+        blocks = pltpu.with_memory_space_constraint(blocks, pltpu.VMEM)
+        n_loads = 2 + 5 * layers + 1
         return pl.pallas_call(
             functools.partial(kernel, group, layers, PARTS, 2 * layers),
             out_shape=pltpu.VMEM((rows, d_model), BF16),
@@ -461,7 +471,7 @@
                 collective_id=0, has_side_effects=True, vmem_limit_bytes=VMEM_MIB * 1024 * 1024),
             cost_estimate=pl.CostEstimate(flops=4 * 10**9, bytes_accessed=64 * 10**6, transcendentals=10**6),
             name="decode_layers",
-        )(attn_first, hidden, lengths.reshape(1, rows), keys, values, attn_norm, w_qkv, w_out, mlp_norm, w_gate, w_up, w_down)
+        )(blocks, hidden, lengths.reshape(1, rows), keys, values, attn_norm, w_qkv, w_out, mlp_norm, w_gate, w_up, w_down)
 
     cache_spec = P(None, "dp", None, "tp", None)
     in_specs = (P("dp", None), P("dp"), cache_spec, cache_spec, P(), P(None, None, "tp", None),

time: 78.5 us -> 72.3 us (0.921)
  Pallas kernels: 77.6 us -> 71.4 us
    pallas_call x1, Pallas kernels: 68.3 us -> 63.4 us  [local_step(): pl.pallas_call(functools.partial(kernel, group, layers, PARTS, 2 * layers...]
    pallas_call x1, Pallas kernels: 9.21 us -> 8 us  [local_step(): pl.pallas_call(functools.partial(first_kernel, group), out_shape=pltpu.VM...]
where the time goes in v5:
time: 72.3 us; the launch traced here: 72.2 us
  Pallas kernels  71.4 us (99%)
  local copies, waits for them, and re-layouts  0.8 us (1%)
    pallas_call x1, Pallas kernels, local_step(): pl.pallas_call(functools.partial(kernel, group, layers, PARTS, 2 * layers...  63.4 us
    pallas_call x1, Pallas kernels, local_step(): pl.pallas_call(functools.partial(first_kernel, group), out_shape=pltpu.VM...  8 us

profile of v5, /device:TPU:81, one launch (start us, length us, event | category | flops | bytes accessed | tf_op | source)
XLA Modules:
  0.0 72.2 jit_solution(13724072109384151252)
XLA Ops:
  0.0 8.0 %first_attention.1.blocks = bf16[2,4,2,64,256]{4,3,2,1,0:T(8,128)(2,1)S(1)} custom-call(bf16[128,2048]{1,0:T(8,128)(2,1)} %hidden.3, s32[1,128]{1,0:T(1,128)} %bitcast.18, s32[128]{0:T(128)} %len_flat.1, bf16[2,128,64,512]{3,2,1,0:T(8,128)(2,1)} %bitcast.12, bf16[2,128,64,512]{3,2,1,0:T(8,128)(2,1)} %bitcast.14, bf16[2,2048]{1,0:T(2,128)(2,1)} %attn_norm.3, ...), custom_call_target="tpu_custom_call" | custom-call | flops 1000000000 | bytes 10000000 | tf_op jit(solution)/shard_map/first_attention/pallas_call | solution.py:402
  8.0 63.4 %decode_layers.1 = bf16[128,2048]{1,0:T(8,128)(2,1)S(1)} custom-call(bf16[2,4,2,64,256]{4,3,2,1,0:T(8,128)(2,1)S(1)} %first_attention.1.blocks, bf16[128,2048]{1,0:T(8,128)(2,1)} %hidden.3, s32[1,128]{1,0:T(1,128)} %bitcast.19, bf16[2,128,64,512]{3,2,1,0:T(8,128)(2,1)} %bitcast.13, bf16[2,128,64,512]{3,2,1,0:T(8,128)(2,1)} %bitcast.15, ...), custom_call_target="tpu_custom_call" | custom-call | flops 4000000000 | bytes 64000000 | tf_op jit(solution)/shard_map/decode_layers/pallas_call | solution.py:434
  71.4 0.8 %copy.15 = bf16[128,2048]{1,0:T(8,128)(2,1)} copy(bf16[128,2048]{1,0:T(8,128)(2,1)S(1)} %decode_layers.1) | data formatting | bytes 1048576

commit v6 on v5

--- a/solution.py
+++ b/solution.py
@@ -32,12 +32,13 @@
     sin_tab[...] = jnp.concatenate([-sine, sine, -sine, sine], axis=0).T
 
 
-def write_normed(normed, part, group, pieces, gain_row):
+def write_normed(normed, part, group, pieces, gain_row, total=None):
     width = normed.shape[1] // group
-    total = jnp.zeros((part.size, 1), F32)
-    for i in range(group):
-        wide = pieces(i)
-        total = total + jnp.sum(wide * wide, axis=1, keepdims=True)
+    if total is None:
+        total = jnp.zeros((part.size, 1), F32)
+        for i in range(group):
+            wide = pieces(i)
+            total = total + jnp.sum(wide * wide, axis=1, keepdims=True)
     scale = lax.rsqrt(total / normed.shape[1] + NORM_EPS)
     for i in range(group):
         cols = slice(i * width, (i + 1) * width)
@@ -287,18 +288,25 @@
             total = total + block_in[p, source].astype(F32)
         xg[me, ranges[p]] = total.astype(BF16)
         mine = xg.at[me, ranges[p]]
-        for index, target in enumerate((far * 2 + core, right * 2 + core, left * 2 + core, sibling)):
+        for index, target in enumerate((far * 2 + core, right * 2 + core, left * 2 + core, right * 2 + other,
+                                        left * 2 + other, sibling)):
             start(p, remote(mine, mine, ag_send.at[p, index], ag_recv.at[p, me], target))
 
     def forward(p):
-        for index, source in enumerate((right * 2 + core, left * 2 + core, far * 2 + core)):
-            piece = xg.at[source, ranges[p]]
-            arrived(piece, ag_recv.at[p, source])
-            start(p, remote(piece, piece, ag_send.at[p, 4 + index], ag_recv.at[p, source], sibling))
-
-    def gathered(p):
-        for source in (sibling, right * 2 + other, left * 2 + other, far * 2 + other):
+        source = far * 2 + core
+        piece = xg.at[source, ranges[p]]
+        arrived(piece, ag_recv.at[p, source])
+        start(p, remote(piece, piece, ag_send.at[p, 6], ag_recv.at[p, source], sibling))
+
+    def gathered(p, look=lambda source: None):
+        look(me)
+        for source in (sibling, right * 2 + core, left * 2 + core, right * 2 + other, left * 2 + other):
             arrived(xg.at[source, ranges[p]], ag_recv.at[p, source])
+            look(source)
+        look(far * 2 + core)
+        source = far * 2 + other
+        arrived(xg.at[source, ranges[p]], ag_recv.at[p, source])
+        look(source)
 
     def compute(p, stage, hook):
         layer, which = stage // 2, stage % 2
@@ -309,8 +317,14 @@
             for index, target in enumerate((far, right, left, chip)):
                 send_blocks(p, index, target, blocks.at[p, target])
             return
-        gathered(p)
-        write_normed(normed, ranges[p], group, lambda i: xg[i, ranges[p]].astype(F32), gain)
+        squares = []
+
+        def look(source):
+            wide = xg[source, ranges[p]].astype(F32)
+            squares.append(jnp.sum(wide * wide, axis=1, keepdims=True))
+
+        gathered(p, look)
+        write_normed(normed, ranges[p], group, lambda i: xg[i, ranges[p]].astype(F32), gain, sum(squares))
         if which == 0:
             if p == 0:
                 ld_q[layer].wait()

time: 72.3 us -> 74.5 us (1.030)
  Pallas kernels: 71.4 us -> 73.6 us
    pallas_call x1, Pallas kernels: 63.4 us -> 65.6 us  [local_step(): pl.pallas_call(functools.partial(kernel, group, layers, PARTS, 2 * layers...]
where the time goes in v6:
time: 74.5 us; the launch traced here: 74.4 us
  Pallas kernels  73.6 us (99%)
  local copies, waits for them, and re-layouts  0.8 us (1%)
    pallas_call x1, Pallas kernels, local_step(): pl.pallas_call(functools.partial(kernel, group, layers, PARTS, 2 * layers...  65.6 us
    pallas_call x1, Pallas kernels, local_step(): pl.pallas_call(functools.partial(first_kernel, group), out_shape=pltpu.VM...  8 us

profile of v6, /device:TPU:81, one launch (start us, length us, event | category | flops | bytes accessed | tf_op | source)
XLA Modules:
  0.0 74.4 jit_solution(1331582900219910778)
XLA Ops:
  0.0 8.0 %first_attention.1.blocks = bf16[2,4,2,64,256]{4,3,2,1,0:T(8,128)(2,1)S(1)} custom-call(bf16[128,2048]{1,0:T(8,128)(2,1)} %hidden.3, s32[1,128]{1,0:T(1,128)} %bitcast.18, s32[128]{0:T(128)} %len_flat.1, bf16[2,128,64,512]{3,2,1,0:T(8,128)(2,1)} %bitcast.12, bf16[2,128,64,512]{3,2,1,0:T(8,128)(2,1)} %bitcast.14, bf16[2,2048]{1,0:T(2,128)(2,1)} %attn_norm.3, ...), custom_call_target="tpu_custom_call" | custom-call | flops 1000000000 | bytes 10000000 | tf_op jit(solution)/shard_map/first_attention/pallas_call | solution.py:416
  8.0 65.6 %decode_layers.1 = bf16[128,2048]{1,0:T(8,128)(2,1)S(1)} custom-call(bf16[2,4,2,64,256]{4,3,2,1,0:T(8,128)(2,1)S(1)} %first_attention.1.blocks, bf16[128,2048]{1,0:T(8,128)(2,1)} %hidden.3, s32[1,128]{1,0:T(1,128)} %bitcast.19, bf16[2,128,64,512]{3,2,1,0:T(8,128)(2,1)} %bitcast.13, bf16[2,128,64,512]{3,2,1,0:T(8,128)(2,1)} %bitcast.15, ...), custom_call_target="tpu_custom_call" | custom-call | flops 4000000000 | bytes 64000000 | tf_op jit(solution)/shard_map/decode_layers/pallas_call | solution.py:448
  73.6 0.8 %copy.15 = bf16[128,2048]{1,0:T(8,128)(2,1)} copy(bf16[128,2048]{1,0:T(8,128)(2,1)S(1)} %decode_layers.1) | data formatting | bytes 1048576

commit v7 on v5

--- a/solution.py
+++ b/solution.py
@@ -34,11 +34,12 @@
 
 def write_normed(normed, part, group, pieces, gain_row):
     width = normed.shape[1] // group
-    total = jnp.zeros((part.size, 1), F32)
+    folded = jnp.zeros((part.size, 128), F32)
     for i in range(group):
         wide = pieces(i)
-        total = total + jnp.sum(wide * wide, axis=1, keepdims=True)
-    scale = lax.rsqrt(total / normed.shape[1] + NORM_EPS)
+        for c in range(0, width, 128):
+            folded = folded + wide[:, c:c + 128] * wide[:, c:c + 128]
+    scale = lax.rsqrt(jnp.sum(folded, axis=1, keepdims=True) / normed.shape[1] + NORM_EPS)
     for i in range(group):
         cols = slice(i * width, (i + 1) * width)
         normed[part, cols] = (pieces(i) * scale * gain_row(cols)).astype(BF16)

time: 72.3 us -> 72 us (level)
  no operation moved by 1% of the time
where the time goes in v7:
time: 72 us
  Pallas kernels  71.2 us (99%)
  local copies, waits for them, and re-layouts  0.8 us (1%)
    pallas_call x1, Pallas kernels, local_step(): pl.pallas_call(functools.partial(kernel, group, layers, PARTS, 2 * layers...  63.1 us
    pallas_call x1, Pallas kernels, local_step(): pl.pallas_call(functools.partial(first_kernel, group), out_shape=pltpu.VM...  8 us

profile of v7, /device:TPU:81, one launch (start us, length us, event | category | flops | bytes accessed | tf_op | source)
XLA Modules:
  0.0 72.0 jit_solution(12451990492242867895)
XLA Ops:
  0.0 8.0 %first_attention.1.blocks = bf16[2,4,2,64,256]{4,3,2,1,0:T(8,128)(2,1)S(1)} custom-call(bf16[128,2048]{1,0:T(8,128)(2,1)} %hidden.3, s32[1,128]{1,0:T(1,128)} %bitcast.18, s32[128]{0:T(128)} %len_flat.1, bf16[2,128,64,512]{3,2,1,0:T(8,128)(2,1)} %bitcast.12, bf16[2,128,64,512]{3,2,1,0:T(8,128)(2,1)} %bitcast.14, bf16[2,2048]{1,0:T(2,128)(2,1)} %attn_norm.3, ...), custom_call_target="tpu_custom_call" | custom-call | flops 1000000000 | bytes 10000000 | tf_op jit(solution)/shard_map/first_attention/pallas_call | solution.py:403
  8.0 63.1 %decode_layers.1 = bf16[128,2048]{1,0:T(8,128)(2,1)S(1)} custom-call(bf16[2,4,2,64,256]{4,3,2,1,0:T(8,128)(2,1)S(1)} %first_attention.1.blocks, bf16[128,2048]{1,0:T(8,128)(2,1)} %hidden.3, s32[1,128]{1,0:T(1,128)} %bitcast.19, bf16[2,128,64,512]{3,2,1,0:T(8,128)(2,1)} %bitcast.13, bf16[2,128,64,512]{3,2,1,0:T(8,128)(2,1)} %bitcast.15, ...), custom_call_target="tpu_custom_call" | custom-call | flops 4000000000 | bytes 64000000 | tf_op jit(solution)/shard_map/decode_layers/pallas_call | solution.py:435
  71.2 0.8 %copy.15 = bf16[128,2048]{1,0:T(8,128)(2,1)} copy(bf16[128,2048]{1,0:T(8,128)(2,1)S(1)} %decode_layers.1) | data formatting | bytes 1048576
